TPU v7x, 32 devices: a whole 2x2x4 slice. The times are simulated.
32 devices in a mesh: rep: 4 (over x, core), shard: 8 (over z, y).
Axes of the slice: x: 2, y: 2, z: 4, core: 2. Of those that a mesh axis runs over, the one named last changes fastest.
Arguments:
- latents: bfloat16 [2, 8, 1024, 1408], P(None, 'shard', 'rep'), may hold values from -6 to 6
- skip_branch: bfloat16 [2, 8, 1024, 1408], P(None, 'shard', 'rep'), may hold values from -6 to 6
- text_states: bfloat16 [2, 8, 256, 1024], P(None, 'shard'), may hold values from -6 to 6
- time_embed: bfloat16 [2, 8, 1408], P(None, 'shard'), may hold values from -6 to 6
- out_cotangent: bfloat16 [2, 8, 1024, 1408], P(None, 'shard', 'rep'), may hold values from -6 to 6
- skip_proj: bfloat16 [2816, 1408], P('shard'), may hold values from -0.109375 to 0.109375
- shift_proj: bfloat16 [1408, 1408], P('shard'), may hold values from -0.15625 to 0.15625
- self_proj_in: bfloat16 [1408, 4224], P('shard'), may hold values from -0.15625 to 0.15625
- self_proj_out: bfloat16 [1408, 1408], P('shard'), may hold values from -3 to 3
- cross_query: bfloat16 [1408, 1408], P('shard'), may hold values from -0.15625 to 0.15625
- cross_keyval: bfloat16 [1024, 2816], P('shard'), may hold values from -0.1875 to 0.1875
- cross_proj_out: bfloat16 [1408, 1408], P('shard'), may hold values from -1.5 to 1.5
- feed_up: bfloat16 [1408, 6144], P('shard'), may hold values from -0.15625 to 0.15625
- feed_down: bfloat16 [6144, 1408], P('shard'), may hold values from -0.078125 to 0.078125
- norm_gains: bfloat16 [5, 1408], P(None, 'shard'), may hold values from 0.5 to 1.5
- bias_rows: bfloat16 [16, 1408], P(None, 'shard'), may hold values from -1.1953125 to 1.1953125
- feed_up_bias: bfloat16 [6144], P('shard'), may hold values from -1.1953125 to 1.1953125
- head_gains: bfloat16 [4, 88], replicated, may hold values from 0.5 to 1.5
- head_biases: bfloat16 [3, 88], replicated, may hold values from -1.1953125 to 1.1953125
Outputs:
- activations: bfloat16 [2, 8, 1024, 1408], P(None, 'shard', 'rep')
- input_grad: float32 [2, 8, 1024, 1408], P(None, 'shard', 'rep')
- skip_grad: float32 [2, 8, 1024, 1408], P(None, 'shard', 'rep')
- text_grad: float32 [2, 8, 256, 1024], P(None, 'shard')
- skip_proj_grad: float32 [2816, 1408], P('shard')
- shift_proj_grad: float32 [1408, 1408], P('shard')
- self_in_grad: float32 [1408, 4224], P('shard')
- self_out_grad: float32 [1408, 1408], P('shard')
- cross_query_grad: float32 [1408, 1408], P('shard')
- cross_keyval_grad: float32 [1024, 2816], P('shard')
- cross_out_grad: float32 [1408, 1408], P('shard')
- feed_up_grad: float32 [1408, 6144], P('shard')
- feed_down_grad: float32 [6144, 1408], P('shard')
- norm_gains_grad: float32 [5, 1408], P(None, 'shard')
- bias_rows_grad: float32 [16, 1408], P(None, 'shard')
- feed_bias_grad: float32 [6144], P('shard')
- head_gains_grad: float32 [4, 88], replicated
- head_biases_grad: float32 [3, 88], replicated
All inputs are finite; a program needn't handle non-finite values.
Results may differ from a plain program's by a relative error of at most 0.019.
Values may be sent and summed in bfloat16 or wider, within the bound.
A program may use at most 336 MiB of HBM per device.

v0:
```python
from functools import partial

import jax
import jax.numpy as jnp
from jax import lax
from jax.sharding import PartitionSpec as P

D = 1408
GRID = 32
MB = 2
HD = 88


def layer_norm(operand, scales, offsets):
    row_mean = jnp.mean(operand, -1, keepdims=True)
    centred = operand - row_mean
    spread = jnp.mean(centred * centred, -1, keepdims=True)
    return centred * lax.rsqrt(spread + 1e-06) * scales + offsets


def rotary_tables(positions):
    pair_index = jnp.arange(HD // 4, dtype=jnp.float32)
    frequency = 10000.0 ** (-2.0 * pair_index / (HD // 2))
    row_coord = (positions // GRID).astype(jnp.float32)
    column_coord = (positions % GRID).astype(jnp.float32)
    angles = jnp.concatenate(
        [row_coord[:, None] * frequency[None, :], column_coord[:, None] * frequency[None, :]],
        axis=1,
    )
    return (jnp.cos(angles), jnp.sin(angles))


def rotate(heads_in, cosine_table, sine_table):
    paired = heads_in.reshape(heads_in.shape[0], heads_in.shape[1], HD // 2, 2)
    even_part = paired[..., 0]
    odd_part = paired[..., 1]
    cosine_rows = cosine_table[:, None, :]
    sine_rows = sine_table[:, None, :]
    turned = jnp.stack(
        [
            even_part * cosine_rows - odd_part * sine_rows,
            even_part * sine_rows + odd_part * cosine_rows,
        ],
        axis=-1,
    )
    return turned.reshape(heads_in.shape)


def head_view(matrix):
    return matrix.reshape(matrix.shape[0], -1, HD)


def product(left_side, right_side):
    return jnp.dot(left_side, right_side, preferred_element_type=jnp.float32)


def weight_grad(left_side, right_side):
    return lax.dot_general(
        left_side, right_side, (((0,), (0,)), ((), ())), preferred_element_type=jnp.float32
    )


def back_product(grad_rows, weight):
    return lax.dot_general(
        grad_rows, weight, (((1,), (1,)), ((), ())), preferred_element_type=jnp.float32
    )


def attend_forward(queries, keys_all, values_all):
    head_count = queries.shape[1]
    per_group = head_count // 4
    score_scale = HD ** (-0.5)

    def one_group(head_start):
        query_part = lax.dynamic_slice_in_dim(queries, head_start, per_group, 1)
        key_part = lax.dynamic_slice_in_dim(keys_all, head_start, per_group, 1)
        value_part = lax.dynamic_slice_in_dim(values_all, head_start, per_group, 1)
        scores = (
            jnp.einsum("qhd,khd->hqk", query_part, key_part, preferred_element_type=jnp.float32)
            * score_scale
        )
        row_max = jnp.max(scores, -1, keepdims=True)
        exponent = jnp.exp(scores - row_max)
        row_sum = jnp.sum(exponent, -1, keepdims=True)
        soft_weights = (exponent / row_sum).astype(jnp.bfloat16)
        mixed_out = jnp.einsum(
            "hqk,khd->qhd", soft_weights, value_part, preferred_element_type=jnp.float32
        )
        return (mixed_out, (row_max + jnp.log(row_sum))[..., 0])

    starts = jnp.arange(4, dtype=jnp.int32) * per_group
    mixed_out, log_total = lax.map(one_group, starts)
    tok_count = queries.shape[0]
    mixed_out = jnp.moveaxis(mixed_out, 0, 1).reshape(tok_count, head_count * HD)
    return (mixed_out, log_total.reshape(head_count, tok_count))


def attend_backward(queries, keys_all, values_all, log_total, grad_mixed):
    head_count = queries.shape[1]
    per_group = head_count // 4
    score_scale = HD ** (-0.5)

    def one_group(head_start):
        query_part = lax.dynamic_slice_in_dim(queries, head_start, per_group, 1)
        key_part = lax.dynamic_slice_in_dim(keys_all, head_start, per_group, 1)
        value_part = lax.dynamic_slice_in_dim(values_all, head_start, per_group, 1)
        grad_part = lax.dynamic_slice_in_dim(grad_mixed, head_start, per_group, 1)
        log_part = lax.dynamic_slice_in_dim(log_total, head_start, per_group, 0)
        scores = (
            jnp.einsum("qhd,khd->hqk", query_part, key_part, preferred_element_type=jnp.float32)
            * score_scale
        )
        soft_weights = jnp.exp(scores - log_part[..., None])
        grad_weights = jnp.einsum(
            "qhd,khd->hqk", grad_part, value_part, preferred_element_type=jnp.float32
        )
        row_inner = jnp.sum(soft_weights * grad_weights, -1, keepdims=True)
        grad_scores = (soft_weights * (grad_weights - row_inner)).astype(jnp.bfloat16)
        grad_query = (
            jnp.einsum("hqk,khd->qhd", grad_scores, key_part, preferred_element_type=jnp.float32)
            * score_scale
        )
        grad_key = (
            jnp.einsum("hqk,qhd->khd", grad_scores, query_part, preferred_element_type=jnp.float32)
            * score_scale
        )
        grad_value = jnp.einsum(
            "hqk,qhd->khd",
            soft_weights.astype(jnp.bfloat16),
            grad_part,
            preferred_element_type=jnp.float32,
        )
        return (grad_query, grad_key, grad_value)

    starts = jnp.arange(4, dtype=jnp.int32) * per_group
    grad_query, grad_key, grad_value = lax.map(one_group, starts)
    grad_query = jnp.moveaxis(grad_query, 0, 1).reshape(queries.shape[0], head_count, HD)
    grad_key = jnp.moveaxis(grad_key, 0, 1).reshape(keys_all.shape[0], head_count, HD)
    grad_value = jnp.moveaxis(grad_value, 0, 1).reshape(keys_all.shape[0], head_count, HD)
    return (grad_query, grad_key, grad_value)


def add_into(store, member, tensor):
    store[member] = tensor if store[member] is None else store[member] + tensor


def shards(
    latents,
    skip_branch,
    text_states,
    time_embed,
    out_cotangent,
    skip_proj,
    shift_proj,
    self_proj_in,
    self_proj_out,
    cross_query,
    cross_keyval,
    cross_proj_out,
    feed_up,
    feed_down,
    norm_gains,
    bias_rows,
    feed_up_bias,
    head_gains,
    head_biases,
):
    local_tokens = latents.shape[2]
    positions = lax.axis_index("rep") * local_tokens + jnp.arange(local_tokens, dtype=jnp.int32)
    cosine_table, sine_table = rotary_tables(positions)
    head_scales = head_gains.astype(jnp.float32)
    head_shifts = head_biases.astype(jnp.float32)

    def self_heads(query_raw, key_raw, gain_query, bias_query, gain_key, bias_key):
        return (
            rotate(
                layer_norm(head_view(query_raw), gain_query, bias_query), cosine_table, sine_table
            ),
            rotate(layer_norm(head_view(key_raw), gain_key, bias_key), cosine_table, sine_table),
        )

    def cross_heads(query_raw, key_raw, gain_query, bias_query, gain_key):
        return (
            layer_norm(head_view(query_raw), gain_query, bias_query),
            layer_norm(head_view(key_raw), gain_key, 0.0),
        )

    totals = [None] * 12
    owned = [None] * 12
    outputs = []
    input_grads = []
    skip_grads = []
    text_grads = []
    head_gain_total = jnp.zeros(head_gains.shape, jnp.float32)
    head_bias_total = jnp.zeros(head_biases.shape, jnp.float32)
    for batch_index in range(MB):
        (
            skip_full,
            shift_full,
            proj_in_full,
            proj_out_full,
            query_full,
            keyval_full,
            cross_out_full,
            up_full,
            down_full,
            gains_full,
            biases_full,
            up_bias_full,
        ) = (
            lax.all_gather(skip_proj, "shard", axis=0, tiled=True),
            lax.all_gather(shift_proj, "shard", axis=0, tiled=True),
            lax.all_gather(self_proj_in, "shard", axis=0, tiled=True),
            lax.all_gather(self_proj_out, "shard", axis=0, tiled=True),
            lax.all_gather(cross_query, "shard", axis=0, tiled=True),
            lax.all_gather(cross_keyval, "shard", axis=0, tiled=True),
            lax.all_gather(cross_proj_out, "shard", axis=0, tiled=True),
            lax.all_gather(feed_up, "shard", axis=0, tiled=True),
            lax.all_gather(feed_down, "shard", axis=0, tiled=True),
            lax.all_gather(norm_gains, "shard", axis=1, tiled=True),
            lax.all_gather(bias_rows, "shard", axis=1, tiled=True),
            lax.all_gather(feed_up_bias, "shard", axis=0, tiled=True),
        )
        gain_rows = gains_full.astype(jnp.float32)
        bias_vals = biases_full.astype(jnp.float32)
        up_offsets = up_bias_full.astype(jnp.float32)
        latent_rows = latents[batch_index, 0].astype(jnp.float32)
        skip_rows = skip_branch[batch_index, 0].astype(jnp.float32)
        text_rows = text_states[batch_index, 0]
        time_row = time_embed[batch_index, 0].astype(jnp.float32)
        joined = jnp.concatenate([latent_rows, skip_rows], axis=1)
        gain_cat = jnp.concatenate([gain_rows[0], gain_rows[1]])
        bias_cat = jnp.concatenate([bias_vals[0], bias_vals[1]])
        normed, joined_pull = jax.vjp(layer_norm, joined, gain_cat, bias_cat)
        normed_low = normed.astype(jnp.bfloat16)
        hidden = product(normed_low, skip_full) + bias_vals[2]
        silu_low = jax.nn.silu(time_row).astype(jnp.bfloat16)
        shift_vec = product(silu_low[None, :], shift_full)[0] + bias_vals[4]
        first_ln, first_pull = jax.vjp(layer_norm, hidden, gain_rows[2], bias_vals[3])
        first_low = (first_ln + shift_vec).astype(jnp.bfloat16)
        projected = product(first_low, proj_in_full) + bias_vals[5:8].reshape(-1)
        query_raw = projected[:, :D]
        key_raw = projected[:, D : 2 * D]
        value_raw = projected[:, 2 * D :]
        (query_rot, key_rot), self_pull = jax.vjp(
            self_heads,
            query_raw,
            key_raw,
            head_scales[0],
            head_shifts[0],
            head_scales[1],
            head_shifts[1],
        )
        query_low = query_rot.astype(jnp.bfloat16)
        key_low = key_rot.reshape(local_tokens, D).astype(jnp.bfloat16)
        value_low = value_raw.astype(jnp.bfloat16)
        keys_seq, values_seq = (
            lax.all_gather(key_low, "rep", axis=0, tiled=True),
            lax.all_gather(value_low, "rep", axis=0, tiled=True),
        )
        self_mixed, self_log = attend_forward(query_low, head_view(keys_seq), head_view(values_seq))
        self_low = self_mixed.astype(jnp.bfloat16)
        hidden_two = hidden + product(self_low, proj_out_full) + bias_vals[8]
        second, second_pull = jax.vjp(layer_norm, hidden_two, gain_rows[3], bias_vals[9])
        second_low = second.astype(jnp.bfloat16)
        query_cross_raw = product(second_low, query_full) + bias_vals[10]
        text_keyval = product(text_rows, keyval_full) + bias_vals[11:13].reshape(-1)
        (cross_queries, text_keys), cross_pull = jax.vjp(
            cross_heads,
            query_cross_raw,
            text_keyval[:, :D],
            head_scales[2],
            head_shifts[2],
            head_scales[3],
        )
        cross_low = cross_queries.astype(jnp.bfloat16)
        text_key_low = text_keys.astype(jnp.bfloat16)
        text_value_low = head_view(text_keyval[:, D:]).astype(jnp.bfloat16)
        cross_mixed, cross_log = attend_forward(cross_low, text_key_low, text_value_low)
        cross_out_low = cross_mixed.astype(jnp.bfloat16)
        hidden_three = hidden_two + product(cross_out_low, cross_out_full) + bias_vals[13]
        third_norm, third_pull = jax.vjp(layer_norm, hidden_three, gain_rows[4], bias_vals[14])
        third_low = third_norm.astype(jnp.bfloat16)
        up_proj = product(third_low, up_full) + up_offsets
        gelu_val, gelu_pull = jax.vjp(partial(jax.nn.gelu, approximate=True), up_proj)
        gelu_low = gelu_val.astype(jnp.bfloat16)
        result = hidden_three + product(gelu_low, down_full) + bias_vals[15]
        outputs.append(result.astype(jnp.bfloat16))
        skip_back, proj_in_back, proj_out_back = (skip_full, proj_in_full, proj_out_full)
        query_back, keyval_back, cross_out_back = (query_full, keyval_full, cross_out_full)
        up_back, down_back = (up_full, down_full)
        keys_back, values_back = (keys_seq, values_seq)
        grad_low = out_cotangent[batch_index, 0]
        grad_out = grad_low.astype(jnp.float32)
        add_into(totals, 8, weight_grad(gelu_low, grad_low))
        grad_gelu = back_product(grad_low, down_back)
        grad_up = gelu_pull(grad_gelu)[0]
        grad_up_low = grad_up.astype(jnp.bfloat16)
        add_into(totals, 7, weight_grad(third_low, grad_up_low))
        grad_third = back_product(grad_up_low, up_back)
        three_part, gain_last, bias_last = third_pull(grad_third)
        grad_three = grad_out + three_part
        grad_three_low = grad_three.astype(jnp.bfloat16)
        add_into(totals, 6, weight_grad(cross_out_low, grad_three_low))
        grad_cross_mixed = back_product(grad_three_low, cross_out_back).astype(jnp.bfloat16)
        grad_cq, grad_tk, grad_tv = attend_backward(
            cross_low, text_key_low, text_value_low, cross_log, head_view(grad_cross_mixed)
        )
        grad_cq_raw, grad_tk_raw, cross_gain_grad, cross_bias_grad, text_gain_grad = cross_pull(
            (grad_cq, grad_tk)
        )
        grad_cq_low = grad_cq_raw.astype(jnp.bfloat16)
        add_into(totals, 4, weight_grad(second_low, grad_cq_low))
        grad_second = back_product(grad_cq_low, query_back)
        grad_keyval = jnp.concatenate([grad_tk_raw, grad_tv.reshape(grad_tv.shape[0], D)], axis=1)
        grad_kv_low = grad_keyval.astype(jnp.bfloat16)
        add_into(totals, 5, weight_grad(text_rows, grad_kv_low))
        text_grads.append(back_product(grad_kv_low, keyval_back))
        two_part, gain_mid, bias_mid = second_pull(grad_second)
        grad_two = grad_three + two_part
        grad_two_low = grad_two.astype(jnp.bfloat16)
        add_into(totals, 3, weight_grad(self_low, grad_two_low))
        grad_self_mixed = back_product(grad_two_low, proj_out_back).astype(jnp.bfloat16)
        grad_query, grad_key_seq, grad_value_seq = attend_backward(
            query_low,
            head_view(keys_back),
            head_view(values_back),
            self_log,
            head_view(grad_self_mixed),
        )
        grad_key_rows, grad_value_rows = (
            lax.psum_scatter(
                grad_key_seq.reshape(-1, D).astype(jnp.bfloat16),
                "rep",
                scatter_dimension=0,
                tiled=True,
            ).astype(jnp.float32),
            lax.psum_scatter(
                grad_value_seq.reshape(-1, D).astype(jnp.bfloat16),
                "rep",
                scatter_dimension=0,
                tiled=True,
            ).astype(jnp.float32),
        )
        (
            grad_q_raw,
            grad_k_raw,
            self_qgain_grad,
            self_qbias_grad,
            self_kgain_grad,
            self_kbias_grad,
        ) = self_pull((grad_query, head_view(grad_key_rows)))
        grad_proj = jnp.concatenate([grad_q_raw, grad_k_raw, grad_value_rows], axis=1)
        grad_proj_low = grad_proj.astype(jnp.bfloat16)
        add_into(totals, 2, weight_grad(first_low, grad_proj_low))
        grad_first = back_product(grad_proj_low, proj_in_back)
        shift_grad_vec = jnp.sum(grad_first, 0)
        add_into(totals, 1, silu_low.astype(jnp.float32)[:, None] * shift_grad_vec[None, :])
        one_part, gain_first, bias_first = first_pull(grad_first)
        grad_hidden = grad_two + one_part
        grad_hidden_low = grad_hidden.astype(jnp.bfloat16)
        add_into(totals, 0, weight_grad(normed_low, grad_hidden_low))
        grad_normed = back_product(grad_hidden_low, skip_back)
        grad_joined, gain_cat_grad, bias_cat_grad = joined_pull(grad_normed)
        input_grads.append(grad_joined[:, :D])
        skip_grads.append(grad_joined[:, D:])
        add_into(
            totals,
            9,
            jnp.stack([gain_cat_grad[:D], gain_cat_grad[D:], gain_first, gain_mid, gain_last]),
        )
        add_into(
            totals,
            10,
            jnp.concatenate(
                [
                    bias_cat_grad.reshape(2, D),
                    jnp.sum(grad_hidden, 0)[None],
                    bias_first[None],
                    shift_grad_vec[None],
                    jnp.sum(grad_proj, 0).reshape(3, D),
                    jnp.sum(grad_two, 0)[None],
                    bias_mid[None],
                    jnp.sum(grad_cq_raw, 0)[None],
                    jnp.sum(grad_keyval, 0).reshape(2, D),
                    jnp.sum(grad_three, 0)[None],
                    bias_last[None],
                    jnp.sum(grad_out, 0)[None],
                ],
                axis=0,
            ),
        )
        add_into(totals, 11, jnp.sum(grad_up, 0))
        head_gain_total = head_gain_total + jnp.stack(
            [self_qgain_grad, self_kgain_grad, cross_gain_grad, text_gain_grad]
        )
        head_bias_total = head_bias_total + jnp.stack(
            [self_qbias_grad, self_kbias_grad, cross_bias_grad]
        )
    owned = (
        lax.psum_scatter(totals[0], "shard", scatter_dimension=0, tiled=True),
        lax.psum_scatter(totals[1], "shard", scatter_dimension=0, tiled=True),
        lax.psum_scatter(totals[2], "shard", scatter_dimension=0, tiled=True),
        lax.psum_scatter(totals[3], "shard", scatter_dimension=0, tiled=True),
        lax.psum_scatter(totals[4], "shard", scatter_dimension=0, tiled=True),
        lax.psum_scatter(totals[5], "shard", scatter_dimension=0, tiled=True),
        lax.psum_scatter(totals[6], "shard", scatter_dimension=0, tiled=True),
        lax.psum_scatter(totals[7], "shard", scatter_dimension=0, tiled=True),
        lax.psum_scatter(totals[8], "shard", scatter_dimension=0, tiled=True),
        lax.psum_scatter(totals[9], "shard", scatter_dimension=1, tiled=True),
        lax.psum_scatter(totals[10], "shard", scatter_dimension=1, tiled=True),
        lax.psum_scatter(totals[11], "shard", scatter_dimension=0, tiled=True),
    )
    text_stack = jnp.stack(text_grads)[:, None]
    summed = (
        lax.psum(owned[0].astype(jnp.bfloat16), "rep").astype(jnp.float32),
        lax.psum(owned[1].astype(jnp.bfloat16), "rep").astype(jnp.float32),
        lax.psum(owned[2].astype(jnp.bfloat16), "rep").astype(jnp.float32),
        lax.psum(owned[3].astype(jnp.bfloat16), "rep").astype(jnp.float32),
        lax.psum(owned[4].astype(jnp.bfloat16), "rep").astype(jnp.float32),
        lax.psum(owned[5].astype(jnp.bfloat16), "rep").astype(jnp.float32),
        lax.psum(owned[6].astype(jnp.bfloat16), "rep").astype(jnp.float32),
        lax.psum(owned[7].astype(jnp.bfloat16), "rep").astype(jnp.float32),
        lax.psum(owned[8].astype(jnp.bfloat16), "rep").astype(jnp.float32),
        lax.psum(owned[9].astype(jnp.bfloat16), "rep").astype(jnp.float32),
        lax.psum(owned[10].astype(jnp.bfloat16), "rep").astype(jnp.float32),
        lax.psum(owned[11].astype(jnp.bfloat16), "rep").astype(jnp.float32),
        lax.psum(text_stack.astype(jnp.bfloat16), "rep").astype(jnp.float32),
    )
    head_sums = lax.psum((head_gain_total, head_bias_total), ("rep", "shard"))
    return (
        jnp.stack(outputs)[:, None],
        jnp.stack(input_grads)[:, None],
        jnp.stack(skip_grads)[:, None],
        summed[12],
        summed[0],
        summed[1],
        summed[2],
        summed[3],
        summed[4],
        summed[5],
        summed[6],
        summed[7],
        summed[8],
        summed[9],
        summed[10],
        summed[11],
        head_sums[0],
        head_sums[1],
    )


def solution(mesh):
    in_specs = (
        P(None, "shard", "rep", None),
        P(None, "shard", "rep", None),
        P(None, "shard", None, None),
        P(None, "shard", None),
        P(None, "shard", "rep", None),
        P("shard", None),
        P("shard", None),
        P("shard", None),
        P("shard", None),
        P("shard", None),
        P("shard", None),
        P("shard", None),
        P("shard", None),
        P("shard", None),
        P(None, "shard"),
        P(None, "shard"),
        P("shard"),
        P(),
        P(),
    )
    out_specs = (
        P(None, "shard", "rep", None),
        P(None, "shard", "rep", None),
        P(None, "shard", "rep", None),
        P(None, "shard", None, None),
        P("shard", None),
        P("shard", None),
        P("shard", None),
        P("shard", None),
        P("shard", None),
        P("shard", None),
        P("shard", None),
        P("shard", None),
        P("shard", None),
        P(None, "shard"),
        P(None, "shard"),
        P("shard"),
        P(),
        P(),
    )
    return jax.shard_map(shards, mesh=mesh, in_specs=in_specs, out_specs=out_specs, check_vma=False)
```

profile of v0, /device:TPU:0, one launch (start us, length us, event | category | flops | bytes accessed | tf_op | source)
XLA Modules:
  0.0 4807.6 jit_solution(16598215577618522813)
XLA Ops:
  10.1 33.0 all-gather.1
  44.6 31.6 all-gather
  89.2 114.0 %all-gather.17.cloned.1.call-done = bf16[2816,1408]{1,0:T(8,128)(2,1)} async-done(((bf16[352,1408]{1,0:T(8,128)(2,1)}), bf16[2816,1408]{1,0:T(8,128)(2,1)}) %all-gather.17.cloned.1.call-update) | async-done | bytes 7929872 | tf_op jit(solution)/shard_map/all_gather | solution.py:211
  214.6 156.7 %all-gather.21.cloned.1.call-done = bf16[1408,4224]{1,0:T(8,128)(2,1)} async-done(((bf16[176,4224]{1,0:T(8,128)(2,1)}), bf16[1408,4224]{1,0:T(8,128)(2,1)}) %all-gather.21.cloned.1.call-update) | async-done | bytes 11894800 | tf_op jit(solution)/shard_map/all_gather | solution.py:213
  447.3 31.1 all-gather.2
  520.1 30.9 while.104
  551.1 41.1 all-gather.27.cloned.1.call-done
  596.6 66.3 %all-gather.31.cloned.1.call-done = bf16[1408,1408]{1,0:T(8,128)(2,1)} async-done(((bf16[176,1408]{1,0:T(8,128)(2,1)}), bf16[1408,1408]{1,0:T(8,128)(2,1)}) %all-gather.31.cloned.1.call-update) | async-done | bytes 3964944 | tf_op jit(solution)/shard_map/all_gather | solution.py:215
  669.5 20.7 all-gather.39.cloned.1.call-done
  694.7 24.3 all-gather.41.cloned.1.call-done
  719.0 31.3 while.106
  767.3 24.8 while.105
  792.1 21.4 while.107
  830.0 294.1 %all-gather.35.cloned.1.call-done = bf16[1408,6144]{1,0:T(8,128)(2,1)} async-done(((bf16[176,6144]{1,0:T(8,128)(2,1)}), bf16[1408,6144]{1,0:T(8,128)(2,1)}) %all-gather.35.cloned.1.call-update) | async-done | bytes 17301520 | tf_op jit(solution)/shard_map/all_gather | solution.py:218
  1124.1 13.4 convolution_add_fusion.7
  1144.6 313.9 %all-gather.37.cloned.1.call-done = bf16[6144,1408]{1,0:T(8,128)(2,1)} async-done(((bf16[768,1408]{1,0:T(8,128)(2,1)}), bf16[6144,1408]{1,0:T(8,128)(2,1)}) %all-gather.37.cloned.1.call-update) | async-done | bytes 17301520 | tf_op jit(solution)/shard_map/all_gather | solution.py:219
  1458.5 14.3 fusion.341
  1472.8 18.8 fusion.173
  1491.6 14.6 fusion.340
  1506.2 14.5 multiply_reduce_fusion.19
  1529.8 35.5 while.108
  1577.6 45.9 while.110
  1671.3 61.2 %while.109 = (s32[]{:T(128)}, f32[4,256,4,88]{1,3,2,0:T(8,128)}, bf16[4,1024,4,88]{1,3,2,0:T(8,128)(2,1)}, bf16[4,1024,4,88]{1,3,2,0:T(8,128)(2,1)}, s32[4]{0:T(...) while((s32[]{:T(128)}, f32[4,256,4,88]{1,3,2,0:T(8,128)}, ...), condition=%wide.region_61.62_spmd, body=%wide.region_59.61_spmd.sunk | while | flops 935779328 | bytes 86636888 | solution.py:136
  1738.7 61.3 %while.111 = (s32[]{:T(128)}, f32[4,256,4,88]{1,3,2,0:T(8,128)}, bf16[4,1024,4,88]{1,3,2,0:T(8,128)(2,1)}, bf16[4,1024,4,88]{1,3,2,0:T(8,128)(2,1)}, s32[4]{0:T(...) while((s32[]{:T(128)}, f32[4,256,4,88]{1,3,2,0:T(8,128)}, ...), condition=%wide.region_83.84_spmd, body=%wide.region_81.83_spmd.sunk | while | flops 935779328 | bytes 86636888 | solution.py:136
  1859.9 9.7 multiply_add_fusion.12
  1952.6 10.6 fusion.305
  1971.6 11.7 multiply_reduce_fusion.21
  2039.1 10.0 convolution_add_fusion.3
  2050.5 13.8 fusion.300
  2064.3 21.4 convolution_add_fusion.2
  2087.1 19.1 fusion.175
  2106.2 26.2 convolution_add_fusion
  2133.8 16.4 fusion.228
  2150.2 27.8 convolution_add_fusion.1
  2197.0 14.2 fusion.167
  2244.2 37.5 all-reduce.8
  2287.0 61.8 %reduce-scatter.40.cloned.1.call-done = f32[176,1408]{1,0:T(8,128)} async-done(((f32[1408,1408]{1,0:T(8,128)}), f32[176,1408]{1,0:T(8,128)}) %reduce-scatter.40.cloned.1.call-update) | async-done | bytes 991248 | tf_op jit(solution)/shard_map/reduce_scatter | solution.py:407
  2350.8 142.3 %reduce-scatter.30.cloned.1.call-done = f32[176,1408]{1,0:T(8,128)} async-done(((f32[1408,1408]{1,0:T(8,128)}), f32[176,1408]{1,0:T(8,128)}) %reduce-scatter.30.cloned.1.call-update) | async-done | bytes 991248 | tf_op jit(solution)/shard_map/reduce_scatter | solution.py:402
  2495.2 193.9 %reduce-scatter.38.cloned.1.call-done = f32[128,2816]{0,1:T(8,128)} async-done(((f32[1024,2816]{0,1:T(8,128)}), f32[128,2816]{0,1:T(8,128)}) %reduce-scatter.38.cloned.1.call-update) | async-done | bytes 1441808 | tf_op jit(solution)/shard_map/reduce_scatter | solution.py:406
  2691.4 268.3 %reduce-scatter.28.cloned.1.call-done = f32[352,1408]{1,0:T(8,128)} async-done(((f32[2816,1408]{1,0:T(8,128)}), f32[352,1408]{1,0:T(8,128)}) %reduce-scatter.28.cloned.1.call-update) | async-done | bytes 1982480 | tf_op jit(solution)/shard_map/reduce_scatter | solution.py:401
  2962.3 382.7 %reduce-scatter.32.cloned.1.call-done = f32[176,4224]{1,0:T(8,128)} async-done(((f32[1408,4224]{1,0:T(8,128)}), f32[176,4224]{1,0:T(8,128)}) %reduce-scatter.32.cloned.1.call-update) | async-done | bytes 2973712 | tf_op jit(solution)/shard_map/reduce_scatter | solution.py:403
  3348.2 553.9 %reduce-scatter.42.cloned.1.call-done = f32[176,6144]{1,0:T(8,128)} async-done(((f32[1408,6144]{1,0:T(8,128)}), f32[176,6144]{1,0:T(8,128)}) %reduce-scatter.42.cloned.1.call-update) | async-done | bytes 4325392 | tf_op jit(solution)/shard_map/reduce_scatter | solution.py:408
  3906.0 553.2 %reduce-scatter.44.cloned.1.call-done = f32[768,1408]{1,0:T(8,128)} async-done(((f32[6144,1408]{1,0:T(8,128)}), f32[768,1408]{1,0:T(8,128)}) %reduce-scatter.44.cloned.1.call-update) | async-done | bytes 4325392 | tf_op jit(solution)/shard_map/reduce_scatter | solution.py:409
  4464.3 13.3 fusion.166
  4480.2 39.6 all-reduce.9
  4529.4 61.5 %reduce-scatter.48.cloned.1.call-done = f32[176,16]{1,0:T(8,128)} async-done(((f32[1408,16]{1,0:T(8,128)}), f32[176,16]{1,0:T(8,128)}) %reduce-scatter.48.cloned.1.call-update) | async-done | bytes 11280
  4591.8 10.2 all-reduce.10
  4603.7 179.6 %all-reduce.14.cloned.1.call-done = (bf16[128,2816]{0,1:T(8,128)(2,1)}, bf16[2,1,256,1024]{3,2,1,0:T(8,128)(2,1)}, bf16[352,1408]{1,0:T(8,128)(2,1)}, bf16[176,1...) async-done(((bf16[128,2816]{0,1:T(8,128)(2,1)}, ...) | async-done | bytes 10555408 | tf_op jit(solution)/shard_map/psum | solution.py:421
  (1577 shorter events, 842.3 us)
Async XLA Ops:
  7.2 78.0 %all-gather.19.cloned.1.call-start = ((), (), s32[]{:S(2)}) async-start(), calls=%async_computation.16 | async-start | bytes 4460544 | tf_op jit(solution)/shard_map/all_gather | solution.py:212
  7.9 195.3 %all-gather.17.cloned.1.call-start = ((), (), s32[]{:S(2)}) async-start(), calls=%async_computation.15 | async-start | bytes 8921088 | tf_op jit(solution)/shard_map/all_gather | solution.py:211
  8.7 362.7 %all-gather.21.cloned.1.call-start = ((), (), s32[]{:S(2)}) async-start(), calls=%async_computation.17 | async-start | bytes 13381632 | tf_op jit(solution)/shard_map/all_gather | solution.py:213
  9.4 470.4 %all-gather.29.cloned.1.call-start = ((), (), s32[]{:S(2)}) async-start(), calls=%async_computation.21 | async-start | bytes 6488064 | tf_op jit(solution)/shard_map/all_gather | solution.py:216
  10.0 497.3 %all-gather.23.cloned.1.call-start = ((), (), s32[]{:S(2)}) async-start(), calls=%async_computation.18 | async-start | bytes 3604480 | tf_op jit(solution)/shard_map/all_gather | solution.py:259
  43.9 343.3 %copy-start.204 = (f32[1408]{0:T(1024)}, f32[1408]{0:T(1024)S(1)}, u32[]{:S(2)}) copy-start(f32[1408]{0:T(1024)S(1)} %get-tuple-element.606) | copy-start | bytes 16900
  77.0 310.2 %copy-start.200 = (f32[1408]{0:T(1024)}, f32[1408]{0:T(1024)S(1)}, u32[]{:S(2)}) copy-start(f32[1408]{0:T(1024)S(1)} %get-tuple-element.612) | copy-start | bytes 16900
  79.7 338.7 %copy-start.214 = (f32[44,2]{1,0:T(8,128)}, f32[44,2]{1,0:T(8,128)S(1)}, u32[]{:S(2)}) copy-start(f32[44,2]{1,0:T(8,128)S(1)} %mul.1626) | copy-start | bytes 1060
  80.0 343.0 %copy-start.216 = (f32[44,2]{1,0:T(8,128)}, f32[44,2]{1,0:T(8,128)S(1)}, u32[]{:S(2)}) copy-start(f32[44,2]{1,0:T(8,128)S(1)} %mul.1608) | copy-start | bytes 1060
  80.3 344.8 %copy-start.194 = (f32[256,44]{0,1:T(8,128)}, f32[256,44]{0,1:T(8,128)S(1)}, u32[]{:S(2)}) copy-start(f32[256,44]{0,1:T(8,128)S(1)} %get-tuple-element.880) | copy-start | bytes 135172
  80.3 344.8 %copy-start.196 = (f32[256,44]{0,1:T(8,128)}, f32[256,44]{0,1:T(8,128)S(1)}, u32[]{:S(2)}) copy-start(f32[256,44]{0,1:T(8,128)S(1)} %get-tuple-element.881) | copy-start | bytes 135172
  88.5 298.6 %copy-start.248 = (f32[1408]{0:T(1024)}, f32[1408]{0:T(1024)S(1)}, u32[]{:S(2)}) copy-start(f32[1408]{0:T(1024)S(1)} %fusion.222) | copy-start | bytes 16900
  89.2 282.2 %copy-start.238 = (f32[1408]{0:T(1024)}, f32[1408]{0:T(1024)S(1)}, u32[]{:S(2)}) copy-start(f32[1408]{0:T(1024)S(1)} %fusion.221) | copy-start | bytes 16900
  209.7 177.5 %copy-start.295 = (f32[256]{0:T(256)}, f32[256]{0:T(256)S(1)}, u32[]{:S(2)}) copy-start(f32[256]{0:T(256)S(1)} %broadcast_multiply_fusion.12) | copy-start | bytes 3076
  214.2 164.4 %copy-start.62 = (f32[256,1408]{1,0:T(8,128)}, f32[256,1408]{1,0:T(8,128)S(1)}, u32[]{:S(2)}) copy-start(f32[256,1408]{1,0:T(8,128)S(1)} %get-tuple-element.947) | copy-start | bytes 4325380
  214.6 172.6 %copy-start.318 = (f32[256]{0:T(256)}, f32[256]{0:T(256)S(1)}, u32[]{:S(2)}) copy-start(f32[256]{0:T(256)S(1)} %fusion.289) | copy-start | bytes 3076
  416.4 103.7 %all-gather.25.cloned.1.call-start = ((), (), s32[]{:S(2)}) async-start(), calls=%async_computation.19 | async-start | bytes 3604480 | tf_op jit(solution)/shard_map/all_gather | solution.py:258
  436.4 155.8 %all-gather.27.cloned.1.call-start = ((), (), s32[]{:S(2)}) async-start(), calls=%async_computation.20 | async-start | bytes 4460544 | tf_op jit(solution)/shard_map/all_gather | solution.py:214
  437.1 225.8 %all-gather.31.cloned.1.call-start = ((), (), s32[]{:S(2)}) async-start(), calls=%async_computation.22 | async-start | bytes 4460544 | tf_op jit(solution)/shard_map/all_gather | solution.py:215
  437.9 252.3 %all-gather.39.cloned.1.call-start = ((), (), s32[]{:S(2)}) async-start(), calls=%async_computation.26 | async-start | bytes 3604480 | tf_op jit(solution)/shard_map/all_gather | solution.py:259
  440.3 278.7 %all-gather.41.cloned.1.call-start = ((), (), s32[]{:S(2)}) async-start(), calls=%async_computation.27 | async-start | bytes 3604480 | tf_op jit(solution)/shard_map/all_gather | solution.py:258
  443.1 379.0 %all-gather.33.cloned.1.call-start = ((), (), s32[]{:S(2)}) async-start(), calls=%async_computation.23 | async-start | bytes 4460544 | tf_op jit(solution)/shard_map/all_gather | solution.py:217
  443.9 680.2 %all-gather.35.cloned.1.call-start = ((), (), s32[]{:S(2)}) async-start(), calls=%async_computation.24 | async-start | bytes 19464192 | tf_op jit(solution)/shard_map/all_gather | solution.py:218
  444.5 1014.1 %all-gather.37.cloned.1.call-start = ((), (), s32[]{:S(2)}) async-start(), calls=%async_computation.25 | async-start | bytes 19464192 | tf_op jit(solution)/shard_map/all_gather | solution.py:219
  445.2 1408.8 %reduce-scatter.20.cloned.1.call-start = ((), (), s32[]{:S(2)}) async-start(), calls=%async_computation.28 | async-start | bytes 3604480 | tf_op jit(solution)/shard_map/reduce_scatter | solution.py:332
  826.2 694.5 %copy-start.51 = (f32[256,1408]{1,0:T(8,128)}, f32[256,1408]{1,0:T(8,128)S(1)}, u32[]{:S(2)}) copy-start(f32[256,1408]{1,0:T(8,128)S(1)} %get-tuple-element.957) | copy-start | bytes 4325380
  826.2 694.5 %copy-start.260 = (f32[256]{0:T(256)}, f32[256]{0:T(256)S(1)}, u32[]{:S(2)}) copy-start(f32[256]{0:T(256)S(1)} %broadcast_multiply_fusion.10) | copy-start | bytes 3076
  829.6 691.2 %copy-start.66 = (f32[256,1408]{1,0:T(8,128)}, f32[256,1408]{1,0:T(8,128)S(1)}, u32[]{:S(2)}) copy-start(f32[256,1408]{1,0:T(8,128)S(1)} %get-tuple-element.955) | copy-start | bytes 4325380
  829.6 294.5 %copy-start.188 = (f32[1408]{0:T(1024)S(1)}, f32[1408]{0:T(1024)}, u32[]{:S(2)}) copy-start(f32[1408]{0:T(1024)} %get-tuple-element.610) | copy-start | bytes 16900
  829.6 294.5 %copy-start.198 = (f32[1408]{0:T(1024)S(1)}, f32[1408]{0:T(1024)}, u32[]{:S(2)}) copy-start(f32[1408]{0:T(1024)} %get-tuple-element.600) | copy-start | bytes 16900
  829.6 691.1 %copy-start.262 = (f32[256]{0:T(256)}, f32[256]{0:T(256)S(1)}, u32[]{:S(2)}) copy-start(f32[256]{0:T(256)S(1)} %broadcast_multiply_fusion.13) | copy-start | bytes 3076
  829.9 690.8 %copy-start.291 = (f32[256]{0:T(256)}, f32[256]{0:T(256)S(1)}, u32[]{:S(2)}) copy-start(f32[256]{0:T(256)S(1)} %fusion.291) | copy-start | bytes 3076
  830.0 690.8 %copy-start.293 = (f32[256]{0:T(256)}, f32[256]{0:T(256)S(1)}, u32[]{:S(2)}) copy-start(f32[256]{0:T(256)S(1)} %fusion.287) | copy-start | bytes 3076
  1732.5 124.4 %reduce-scatter.24.cloned.1.call-start = ((), (), s32[]{:S(2)}) async-start(), calls=%async_computation.30 | async-start | bytes 3604480 | tf_op jit(solution)/shard_map/reduce_scatter | solution.py:332
  1800.0 141.9 %reduce-scatter.26.cloned.1.call-start = ((), (), s32[]{:S(2)}) async-start(), calls=%async_computation.31 | async-start | bytes 3604480 | tf_op jit(solution)/shard_map/reduce_scatter | solution.py:338
  1804.7 138.5 %reduce-scatter.22.cloned.1.call-start = ((), (), s32[]{:S(2)}) async-start(), calls=%async_computation.29 | async-start | bytes 3604480 | tf_op jit(solution)/shard_map/reduce_scatter | solution.py:338
  1809.9 473.0 %reduce-scatter.34.cloned.1.call-start = ((), (), s32[]{:S(2)}) async-start(), calls=%async_computation.35 | async-start | bytes 8921088 | tf_op jit(solution)/shard_map/reduce_scatter | solution.py:404
  1817.3 467.6 %reduce-scatter.36.cloned.1.call-start = ((), (), s32[]{:S(2)}) async-start(), calls=%async_computation.36 | async-start | bytes 8921088 | tf_op jit(solution)/shard_map/reduce_scatter | solution.py:405
  1826.9 521.8 %reduce-scatter.40.cloned.1.call-start = ((), (), s32[]{:S(2)}) async-start(), calls=%async_computation.38 | async-start | bytes 8921088 | tf_op jit(solution)/shard_map/reduce_scatter | solution.py:407
  1836.0 657.2 %reduce-scatter.30.cloned.1.call-start = ((), (), s32[]{:S(2)}) async-start(), calls=%async_computation.33 | async-start | bytes 8921088 | tf_op jit(solution)/shard_map/reduce_scatter | solution.py:402
  1987.6 701.6 %reduce-scatter.38.cloned.1.call-start = ((), (), s32[]{:S(2)}) async-start(), calls=%async_computation.37 | async-start | bytes 12976128 | tf_op jit(solution)/shard_map/reduce_scatter | solution.py:406
  2029.7 930.1 %reduce-scatter.28.cloned.1.call-start = ((), (), s32[]{:S(2)}) async-start(), calls=%async_computation.32 | async-start | bytes 17842176 | tf_op jit(solution)/shard_map/reduce_scatter | solution.py:401
  2049.2 1295.9 %reduce-scatter.32.cloned.1.call-start = ((), (), s32[]{:S(2)}) async-start(), calls=%async_computation.34 | async-start | bytes 26763264 | tf_op jit(solution)/shard_map/reduce_scatter | solution.py:403
  2085.8 1816.3 %reduce-scatter.42.cloned.1.call-start = ((), (), s32[]{:S(2)}) async-start(), calls=%async_computation.39 | async-start | bytes 38928384 | tf_op jit(solution)/shard_map/reduce_scatter | solution.py:408
  2132.4 2326.8 %reduce-scatter.44.cloned.1.call-start = ((), (), s32[]{:S(2)}) async-start(), calls=%async_computation.40 | async-start | bytes 38928384 | tf_op jit(solution)/shard_map/reduce_scatter | solution.py:409
  2178.1 2350.3 %reduce-scatter.46.cloned.1.call-start = ((), (), s32[]{:S(2)}) async-start(), calls=%async_computation.41 | async-start | bytes 811008
  2232.3 2358.5 %reduce-scatter.48.cloned.1.call-start = ((), (), s32[]{:S(2)}) async-start(), calls=%async_computation.42 | async-start | bytes 811008
  2236.9 2546.4 %all-reduce.14.cloned.1.call-start = ((), (), s32[]{:S(2)}) async-start(), calls=%async_computation.43 | async-start | bytes 21110784 | tf_op jit(solution)/shard_map/psum | solution.py:421
  (402 other events, 4106.6 us)
Sparse Core Ops, SparseCore 0:
  10.2 73.3 all-gather.18
  85.8 117.4 all-gather.16
  205.4 165.8 all-gather.20
  373.4 90.5 all-gather.28
  466.0 25.2 all-gather.22
  492.7 27.3 all-gather.24
  522.3 69.8 all-gather.26
  594.4 68.5 all-gather.30
  664.5 25.6 all-gather.38
  691.6 27.3 all-gather.40
  721.2 69.8 all-gather.32
  792.5 331.5 all-gather.34
  1125.6 332.8 all-gather.36
  1732.6 35.9 reduce-scatter.19
  1800.2 36.1 reduce-scatter.23
  1839.3 36.1 reduce-scatter.25
  1877.9 36.1 reduce-scatter.21
  1917.7 141.6 reduce-scatter.33
  2063.0 140.7 reduce-scatter.35
  2207.3 141.4 reduce-scatter.39
  2352.4 140.7 reduce-scatter.29
  2496.8 192.3 reduce-scatter.37
  2693.1 266.6 reduce-scatter.27
  2963.5 381.5 reduce-scatter.31
  3348.9 553.1 reduce-scatter.41
  3905.8 553.2 reduce-scatter.43
  4462.9 62.3 reduce-scatter.45
  4528.6 62.2 reduce-scatter.47
  4595.6 187.6 all-reduce.13
where the time goes:
time: 4820 us; the launch traced here: 4810 us
  waiting for transfers between devices  3440 us (71%)
  matrix products  577 us (12%)
  local copies, waits for them, and re-layouts  292 us (6%)
  other arithmetic  226 us (5%)
  blocking collectives  183 us (4%)
  loops' own time  63.8 us (1%)
    reduce_scatter x1, waiting for transfers between devices, shards(): lax.psum_scatter(totals[7], 'shard', scatter_dimension=0, tiled=True)  554 us
    reduce_scatter x1, waiting for transfers between devices, shards(): lax.psum_scatter(totals[8], 'shard', scatter_dimension=0, tiled=True)  553 us
    reduce_scatter x1, waiting for transfers between devices, shards(): lax.psum_scatter(totals[2], 'shard', scatter_dimension=0, tiled=True)  383 us
    all_gather x1, waiting for transfers between devices, shards(): lax.all_gather(feed_down, 'shard', axis=0, tiled=True)  314 us
    all_gather x1, waiting for transfers between devices, shards(): lax.all_gather(feed_up, 'shard', axis=0, tiled=True)  294 us
    reduce_scatter x1, waiting for transfers between devices, shards(): lax.psum_scatter(totals[0], 'shard', scatter_dimension=0, tiled=True)  268 us
    reduce_scatter x1, waiting for transfers between devices, shards(): lax.psum_scatter(totals[5], 'shard', scatter_dimension=0, tiled=True)  194 us
    psum x1, waiting for transfers between devices, shards(): lax.psum(owned[5].astype(jnp.bfloat16), 'rep').astype(jnp.float32)  180 us
  transfers between devices with their start and end apart: 29, of which 18 were waited for; matrix products, arithmetic and copies ran while one was open for 16% of the time, Pallas kernels for 0%

commit v1 on v0

v1 whole, which is shorter than its diff:
```python
from functools import partial

import jax
import jax.numpy as jnp
import numpy as np
from jax import lax
from jax.experimental import pallas as pl
from jax.experimental.pallas import tpu as pltpu
from jax.sharding import PartitionSpec as P

D = 1408
GRID = 32
MB = 2
HD = 88


def layer_norm(operand, scales, offsets):
    row_mean = jnp.mean(operand, -1, keepdims=True)
    centred = operand - row_mean
    spread = jnp.mean(centred * centred, -1, keepdims=True)
    return centred * lax.rsqrt(spread + 1e-06) * scales + offsets


def rotary_tables(positions):
    pair_index = jnp.arange(HD // 4, dtype=jnp.float32)
    frequency = 10000.0 ** (-2.0 * pair_index / (HD // 2))
    row_coord = (positions // GRID).astype(jnp.float32)
    column_coord = (positions % GRID).astype(jnp.float32)
    angles = jnp.concatenate(
        [row_coord[:, None] * frequency[None, :], column_coord[:, None] * frequency[None, :]],
        axis=1,
    )
    return (jnp.cos(angles), jnp.sin(angles))


def rotate(heads_in, cosine_table, sine_table):
    paired = heads_in.reshape(heads_in.shape[0], heads_in.shape[1], HD // 2, 2)
    even_part = paired[..., 0]
    odd_part = paired[..., 1]
    cosine_rows = cosine_table[:, None, :]
    sine_rows = sine_table[:, None, :]
    turned = jnp.stack(
        [
            even_part * cosine_rows - odd_part * sine_rows,
            even_part * sine_rows + odd_part * cosine_rows,
        ],
        axis=-1,
    )
    return turned.reshape(heads_in.shape)


def head_view(matrix):
    return matrix.reshape(matrix.shape[0], -1, HD)


def product(left_side, right_side):
    return jnp.dot(left_side, right_side, preferred_element_type=jnp.float32)


def weight_grad(left_side, right_side):
    return lax.dot_general(
        left_side, right_side, (((0,), (0,)), ((), ())), preferred_element_type=jnp.float32
    )


def back_product(grad_rows, weight):
    return lax.dot_general(
        grad_rows, weight, (((1,), (1,)), ((), ())), preferred_element_type=jnp.float32
    )


def attend_forward(queries, keys_all, values_all):
    head_count = queries.shape[1]
    per_group = head_count // 4
    score_scale = HD ** (-0.5)

    def one_group(head_start):
        query_part = lax.dynamic_slice_in_dim(queries, head_start, per_group, 1)
        key_part = lax.dynamic_slice_in_dim(keys_all, head_start, per_group, 1)
        value_part = lax.dynamic_slice_in_dim(values_all, head_start, per_group, 1)
        scores = (
            jnp.einsum("qhd,khd->hqk", query_part, key_part, preferred_element_type=jnp.float32)
            * score_scale
        )
        row_max = jnp.max(scores, -1, keepdims=True)
        exponent = jnp.exp(scores - row_max)
        row_sum = jnp.sum(exponent, -1, keepdims=True)
        soft_weights = (exponent / row_sum).astype(jnp.bfloat16)
        mixed_out = jnp.einsum(
            "hqk,khd->qhd", soft_weights, value_part, preferred_element_type=jnp.float32
        )
        return (mixed_out, (row_max + jnp.log(row_sum))[..., 0])

    starts = jnp.arange(4, dtype=jnp.int32) * per_group
    mixed_out, log_total = lax.map(one_group, starts)
    tok_count = queries.shape[0]
    mixed_out = jnp.moveaxis(mixed_out, 0, 1).reshape(tok_count, head_count * HD)
    return (mixed_out, log_total.reshape(head_count, tok_count))


def attend_backward(queries, keys_all, values_all, log_total, grad_mixed):
    head_count = queries.shape[1]
    per_group = head_count // 4
    score_scale = HD ** (-0.5)

    def one_group(head_start):
        query_part = lax.dynamic_slice_in_dim(queries, head_start, per_group, 1)
        key_part = lax.dynamic_slice_in_dim(keys_all, head_start, per_group, 1)
        value_part = lax.dynamic_slice_in_dim(values_all, head_start, per_group, 1)
        grad_part = lax.dynamic_slice_in_dim(grad_mixed, head_start, per_group, 1)
        log_part = lax.dynamic_slice_in_dim(log_total, head_start, per_group, 0)
        scores = (
            jnp.einsum("qhd,khd->hqk", query_part, key_part, preferred_element_type=jnp.float32)
            * score_scale
        )
        soft_weights = jnp.exp(scores - log_part[..., None])
        grad_weights = jnp.einsum(
            "qhd,khd->hqk", grad_part, value_part, preferred_element_type=jnp.float32
        )
        row_inner = jnp.sum(soft_weights * grad_weights, -1, keepdims=True)
        grad_scores = (soft_weights * (grad_weights - row_inner)).astype(jnp.bfloat16)
        grad_query = (
            jnp.einsum("hqk,khd->qhd", grad_scores, key_part, preferred_element_type=jnp.float32)
            * score_scale
        )
        grad_key = (
            jnp.einsum("hqk,qhd->khd", grad_scores, query_part, preferred_element_type=jnp.float32)
            * score_scale
        )
        grad_value = jnp.einsum(
            "hqk,qhd->khd",
            soft_weights.astype(jnp.bfloat16),
            grad_part,
            preferred_element_type=jnp.float32,
        )
        return (grad_query, grad_key, grad_value)

    starts = jnp.arange(4, dtype=jnp.int32) * per_group
    grad_query, grad_key, grad_value = lax.map(one_group, starts)
    grad_query = jnp.moveaxis(grad_query, 0, 1).reshape(queries.shape[0], head_count, HD)
    grad_key = jnp.moveaxis(grad_key, 0, 1).reshape(keys_all.shape[0], head_count, HD)
    grad_value = jnp.moveaxis(grad_value, 0, 1).reshape(keys_all.shape[0], head_count, HD)
    return (grad_query, grad_key, grad_value)


def uninitialised(shape, dtype):
    return pl.pallas_call(
        lambda out_ref: None,
        out_shape=jax.ShapeDtypeStruct(shape, dtype),
        out_specs=pl.BlockSpec(memory_space=pl.ANY),
        compiler_params=pltpu.CompilerParams(has_side_effects=True),
    )()


class Links:
    def __init__(self, shard_count, rep_count):
        self.n = shard_count
        self.reps = rep_count
        self.ring = shard_count == 8 and rep_count == 4
        self.half = shard_count // 2
        order = list(range(0, shard_count, 2)) + list(range(shard_count - 1, 0, -2))
        self.order = np.asarray(order, np.int32)
        self.shard = lax.axis_index("shard")
        rep = lax.axis_index("rep")
        self.core = rep % 2
        self.side = rep // 2
        self.sign = 1 - 2 * self.core
        self.position = jnp.asarray(np.argsort(order).astype(np.int32))[self.shard]
        perm = []
        for r in range(rep_count):
            for q in range(shard_count):
                step = 1 if r % 2 == 0 else -1
                perm.append(
                    (
                        r * shard_count + order[q],
                        r * shard_count + order[(q + step) % shard_count],
                    )
                )
        self.ring_perm = perm
        self.core_perm = [(r, r ^ 1) for r in range(rep_count)]
        self.side_perm = [(r, r ^ 2) for r in range(rep_count)]
        self.sent = []

    def at(self, distance):
        return jnp.asarray(self.order)[(self.position + distance + 2 * self.n) % self.n]

    def along_ring(self, block, depth=2):
        if len(self.sent) >= depth:
            block, _ = lax.optimization_barrier((block, self.sent[-depth]))
        moved = lax.ppermute(block, ("rep", "shard"), self.ring_perm)
        self.sent.append(moved)
        return moved

    def swap_core(self, block):
        return lax.ppermute(block, "rep", self.core_perm)

    def swap_side(self, block):
        return lax.ppermute(block, "rep", self.side_perm)


def pick(stack, index):
    return lax.dynamic_index_in_dim(stack, index, 0, keepdims=False)


def place(stack, block, index, row=0):
    return lax.dynamic_update_slice(stack, block[None], (index, row, 0))


def gather_steps(links, piece):
    arrived = []
    block = piece
    for _ in range(1, links.half):
        block = yield block
        arrived.append(block)
    rows = piece.shape[0] // 2
    last = lax.dynamic_slice_in_dim(block, links.core * rows, rows, 0)
    arrived.append((yield last))
    return arrived


def run_steps(links, generators, sequence):
    waiting = {name: next(gen) for name, gen in generators.items()}
    results = {}
    for name in sequence:
        moved = links.along_ring(waiting[name])
        try:
            waiting[name] = generators[name].send(moved)
        except StopIteration as stop:
            results[name] = stop.value
    return results


def lots(arrived):
    return [jnp.concatenate(arrived[:2], 0), jnp.concatenate(arrived[2:], 0)]


def unlots(pair, rows):
    first, second = pair
    return [first[:rows], first[rows:], second[:rows], second[rows:]]


def store_arrivals(links, stack, own, mine, other, row_range):
    low, high = row_range
    total = own.shape[0]
    rows = total // 2
    width = high - low
    stack = place(stack, own[low:high], links.shard)
    for k in range(1, links.half):
        stack = place(stack, mine[k - 1][low:high], links.at(-links.sign * k))
        stack = place(stack, other[k - 1][low:high], links.at(links.sign * k))
    far = links.at(links.half)
    both = jnp.where(
        links.core == 0,
        jnp.concatenate([mine[-1], other[-1]], 0),
        jnp.concatenate([other[-1], mine[-1]], 0),
    )
    stack = place(stack, both[low:high], far)
    return stack


def gather_finish(links, own, arrived, parts):
    rows = own.shape[0]
    other = unlots([links.swap_core(lot) for lot in lots(arrived)], rows)
    wholes = []
    for low, high in parts:
        stack = uninitialised((links.n, high - low, own.shape[1]), own.dtype)
        wholes.append(store_arrivals(links, stack, own, arrived, other, (low, high)))
    return wholes


def gather_finish_halved(links, own, far_own, arrived):
    rows = own.shape[0]
    whole = (0, rows)
    pair = lots(arrived)
    far_pair = [links.swap_side(lot) for lot in pair]
    other, far_other = [], []
    for near_lot, far_lot in zip(pair, far_pair):
        moved = links.swap_core(jnp.concatenate([near_lot, far_lot], 0))
        other.append(moved[: near_lot.shape[0]])
        far_other.append(moved[near_lot.shape[0] :])
    shape = (links.n, rows, own.shape[1])
    near = store_arrivals(
        links, uninitialised(shape, own.dtype), own, arrived, unlots(other, rows), whole
    )
    far = store_arrivals(
        links,
        uninitialised(shape, own.dtype),
        far_own,
        unlots(far_pair, rows),
        unlots(far_other, rows),
        whole,
    )
    return near, far


def total32(*terms):
    total = terms[0].astype(jnp.float32)
    for term in terms[1:]:
        total = total + term.astype(jnp.float32)
    return total


def handled(links, stack, sign):
    blocks = [pick(stack, links.at(sign * k)) for k in range(1, links.half)]
    rows = stack.shape[1] // 2
    core = jnp.where(sign == links.sign, links.core, 1 - links.core)
    blocks.append(lax.dynamic_slice_in_dim(pick(stack, links.at(links.half)), core * rows, rows, 0))
    return blocks


def reduce_ring(links, blocks):
    rows = blocks[-1].shape[0]
    moved = yield blocks[-1]
    top = jnp.zeros_like(moved)
    full = jnp.where(
        links.core == 0,
        jnp.concatenate([moved, top], 0),
        jnp.concatenate([top, moved], 0),
    )
    for k in range(links.half - 1, 0, -1):
        full = yield total32(blocks[k - 1], full).astype(jnp.bfloat16)
    return full


def reduce_start(links, stack):
    rows = stack.shape[1]
    out = jnp.concatenate(handled(links, stack, -links.sign), 0)
    got = links.swap_core(out)
    mine = handled(links, stack, links.sign)
    blocks = []
    for k, block in enumerate(mine):
        part = got[k * rows : k * rows + block.shape[0]]
        blocks.append(total32(block, part).astype(jnp.bfloat16))
    return blocks


def reduce_finish(links, stack, moved):
    rows = stack.shape[1]
    mine = total32(pick(stack, links.shard), moved).astype(jnp.bfloat16)
    chip = total32(mine, links.swap_core(mine)).astype(jnp.bfloat16)
    half = lax.dynamic_slice_in_dim(chip, links.core * (rows // 2), rows // 2, 0)
    half = total32(half, links.swap_side(half)).astype(jnp.bfloat16)
    other = links.swap_core(half)
    return jnp.where(
        links.core == 0,
        jnp.concatenate([half, other], 0),
        jnp.concatenate([other, half], 0),
    ).astype(jnp.float32)


def reduce_start_halved(links, near, far):
    rows = near.shape[1]
    near_blocks = reduce_start_list(links, [near, far])
    mine, theirs = near_blocks
    out = jnp.concatenate(theirs + [pick(far, links.shard)], 0)
    got = links.swap_side(out)
    blocks = []
    for k, block in enumerate(mine):
        part = got[k * rows : k * rows + block.shape[0]]
        blocks.append(total32(block, part).astype(jnp.bfloat16))
    return blocks, got[-rows:]


def reduce_start_list(links, stacks):
    rows = stacks[0].shape[1]
    sends = [jnp.concatenate(handled(links, stack, -links.sign), 0) for stack in stacks]
    got = links.swap_core(jnp.concatenate(sends, 0))
    results = []
    for j, stack in enumerate(stacks):
        base = j * sends[0].shape[0]
        blocks = []
        for k, block in enumerate(handled(links, stack, links.sign)):
            part = got[base + k * rows : base + k * rows + block.shape[0]]
            blocks.append(total32(block, part).astype(jnp.bfloat16))
        results.append(blocks)
    return results


def reduce_finish_halved(links, near, own_far, moved):
    mine = total32(pick(near, links.shard), own_far, moved).astype(jnp.bfloat16)
    total = total32(mine, links.swap_core(mine)).astype(jnp.bfloat16)
    other = links.swap_side(total)
    first = jnp.where(links.side == 0, total, other).astype(jnp.float32)
    second = jnp.where(links.side == 0, other, total).astype(jnp.float32)
    return first, second


def shards(
    shard_count,
    rep_count,
    latents,
    skip_branch,
    text_states,
    time_embed,
    out_cotangent,
    skip_proj,
    shift_proj,
    self_proj_in,
    self_proj_out,
    cross_query,
    cross_keyval,
    cross_proj_out,
    feed_up,
    feed_down,
    norm_gains,
    bias_rows,
    feed_up_bias,
    head_gains,
    head_biases,
):
    links = Links(shard_count, rep_count)
    n = shard_count
    batches, _, local_tokens, _ = latents.shape
    rows_all = batches * local_tokens
    hidden_units = feed_up.shape[1]
    slab = feed_down.shape[0] // 2
    own_rows = shift_proj.shape[0]
    text_depth = cross_keyval.shape[0]
    positions = lax.axis_index("rep") * local_tokens + jnp.arange(local_tokens, dtype=jnp.int32)
    positions = jnp.tile(positions, batches)
    cosine_table, sine_table = rotary_tables(positions)
    head_scales = head_gains.astype(jnp.float32)
    head_shifts = head_biases.astype(jnp.float32)

    def self_heads(query_raw, key_raw, gain_query, bias_query, gain_key, bias_key):
        return (
            rotate(
                layer_norm(head_view(query_raw), gain_query, bias_query), cosine_table, sine_table
            ),
            rotate(layer_norm(head_view(key_raw), gain_key, bias_key), cosine_table, sine_table),
        )

    def cross_heads(query_raw, key_raw, gain_query, bias_query, gain_key):
        return (
            layer_norm(head_view(query_raw), gain_query, bias_query),
            layer_norm(head_view(key_raw), gain_key, 0.0),
        )

    silu_own = jax.nn.silu(time_embed[:, 0].astype(jnp.float32)).astype(jnp.bfloat16)
    flat = jnp.concatenate(
        [norm_gains.reshape(-1), bias_rows.reshape(-1), feed_up_bias, silu_own.reshape(-1)]
    )
    vectors = lax.all_gather(flat[None], "shard", axis=0, tiled=True)
    cut_a = norm_gains.size
    cut_b = cut_a + bias_rows.size
    cut_c = cut_b + feed_up_bias.size
    gain_rows = jnp.moveaxis(vectors[:, :cut_a].reshape(n, norm_gains.shape[0], -1), 0, 1)
    gain_rows = gain_rows.reshape(norm_gains.shape[0], D).astype(jnp.float32)
    bias_vals = jnp.moveaxis(vectors[:, cut_a:cut_b].reshape(n, bias_rows.shape[0], -1), 0, 1)
    bias_vals = bias_vals.reshape(bias_rows.shape[0], D).astype(jnp.float32)
    up_offsets = vectors[:, cut_b:cut_c].astype(jnp.float32).reshape(n, 2, slab)
    silu_all = vectors[:, cut_c:].reshape(n * batches, D)

    silu_cols = lax.dynamic_slice_in_dim(silu_all, links.shard * own_rows, own_rows, 1)
    shift_terms = product(silu_cols, shift_proj).reshape(n, batches, D)
    shift_own = lax.psum_scatter(shift_terms, "shard", scatter_dimension=0, tiled=True)[0]
    shift_vec = shift_own + bias_vals[4]

    up_split = feed_up.reshape(own_rows, n, 2, slab)
    up_near = lax.dynamic_index_in_dim(up_split, links.side, 2, keepdims=False).reshape(own_rows, -1)
    up_far = lax.dynamic_index_in_dim(up_split, 1 - links.side, 2, keepdims=False)
    up_far = up_far.reshape(own_rows, -1)
    down_near = lax.dynamic_slice_in_dim(feed_down, links.side * slab, slab, 0)
    down_far = lax.dynamic_slice_in_dim(feed_down, (1 - links.side) * slab, slab, 0)
    keyval_rows = jnp.concatenate([cross_keyval[:, :D], cross_keyval[:, D:]], 0)
    small = jnp.concatenate([self_proj_out, cross_query, cross_proj_out, keyval_rows], 0)
    cuts = [0, own_rows, 2 * own_rows, 3 * own_rows, 3 * own_rows + text_depth]
    cuts.append(cuts[-1] + text_depth)
    small_parts = list(zip(cuts[:-1], cuts[1:]))
    if links.ring:
        arrivals = run_steps(
            links,
            {
                "skip": gather_steps(links, skip_proj),
                "in": gather_steps(links, self_proj_in),
                "small": gather_steps(links, small),
                "up": gather_steps(links, up_near),
                "down": gather_steps(links, down_near),
            },
            ["skip", "in"] * 4
            + ["up", "small", "up", "small", "up", "small", "up", "down"]
            + ["small", "down", "down", "down"],
        )
        (skip_stack,) = gather_finish(links, skip_proj, arrivals["skip"], [(0, skip_proj.shape[0])])
        (in_stack,) = gather_finish(links, self_proj_in, arrivals["in"], [(0, own_rows)])
        small_stacks = gather_finish(links, small, arrivals["small"], small_parts)
        up_stacks = gather_finish_halved(links, up_near, up_far, arrivals["up"])
        down_stacks = gather_finish_halved(links, down_near, down_far, arrivals["down"])
    else:

        def whole(block):
            return lax.all_gather(block, "shard", axis=0)

        skip_stack, in_stack = whole(skip_proj), whole(self_proj_in)
        small_stacks = [whole(small[low:high]) for low, high in small_parts]
        up_stacks = (whole(up_near), whole(up_far))
        down_stacks = (whole(down_near), whole(down_far))
    skip_full = skip_stack.reshape(-1, D)
    proj_in_full = in_stack.reshape(D, -1)
    proj_out_full = small_stacks[0].reshape(D, D)
    query_full = small_stacks[1].reshape(D, D)
    cross_out_full = small_stacks[2].reshape(D, D)
    text_key_full = small_stacks[3].reshape(-1, D)
    text_value_full = small_stacks[4].reshape(-1, D)
    up_halves = [stack.reshape(D, -1) for stack in up_stacks]
    down_halves = [stack.reshape(-1, D) for stack in down_stacks]
    up_bias_halves = [
        lax.dynamic_index_in_dim(up_offsets, side, 1, keepdims=False).reshape(-1)
        for side in (links.side, 1 - links.side)
    ]

    latent_rows = latents.reshape(rows_all, D).astype(jnp.float32)
    skip_rows = skip_branch.reshape(rows_all, D).astype(jnp.float32)
    text_rows = text_states.reshape(-1, text_states.shape[-1])
    joined = jnp.concatenate([latent_rows, skip_rows], axis=1)
    gain_cat = jnp.concatenate([gain_rows[0], gain_rows[1]])
    bias_cat = jnp.concatenate([bias_vals[0], bias_vals[1]])
    normed, joined_pull = jax.vjp(layer_norm, joined, gain_cat, bias_cat)
    normed_low = normed.astype(jnp.bfloat16)
    hidden = product(normed_low, skip_full) + bias_vals[2]
    first_ln, first_pull = jax.vjp(layer_norm, hidden, gain_rows[2], bias_vals[3])
    first_low = (first_ln.reshape(batches, local_tokens, D) + shift_vec[:, None]).reshape(
        rows_all, D
    )
    first_low = first_low.astype(jnp.bfloat16)
    projected = product(first_low, proj_in_full) + bias_vals[5:8].reshape(-1)
    query_raw = projected[:, :D]
    key_raw = projected[:, D : 2 * D]
    value_raw = projected[:, 2 * D :]
    (query_rot, key_rot), self_pull = jax.vjp(
        self_heads,
        query_raw,
        key_raw,
        head_scales[0],
        head_shifts[0],
        head_scales[1],
        head_shifts[1],
    )
    query_low = query_rot.astype(jnp.bfloat16)
    key_low = key_rot.reshape(rows_all, D).astype(jnp.bfloat16)
    value_low = value_raw.astype(jnp.bfloat16)
    keyval_own = jnp.stack([key_low, value_low])
    if links.ring:
        keyval_side = links.swap_side(keyval_own)
        keyval_core = links.swap_core(keyval_own)
        keyval_both = links.swap_core(keyval_side)
        slots = jnp.stack([keyval_own, keyval_core, keyval_side, keyval_both])
    else:
        slots = lax.all_gather(keyval_own, "rep", axis=0)
    slots = slots.reshape(rep_count, 2, batches, local_tokens, D)

    def batch_of(tensor, index):
        step = tensor.shape[0] // batches
        return tensor[index * step : (index + 1) * step]

    self_saved = []
    self_parts = []
    for b in range(batches):
        keys_seq = head_view(slots[:, 0, b].reshape(-1, D))
        values_seq = head_view(slots[:, 1, b].reshape(-1, D))
        query_part = batch_of(query_low, b)
        mixed, log_total = attend_forward(query_part, keys_seq, values_seq)
        self_saved.append((query_part, keys_seq, values_seq, log_total))
        self_parts.append(mixed.astype(jnp.bfloat16))
    self_low = jnp.concatenate(self_parts, 0)
    hidden_two = hidden + product(self_low, proj_out_full) + bias_vals[8]
    second, second_pull = jax.vjp(layer_norm, hidden_two, gain_rows[3], bias_vals[9])
    second_low = second.astype(jnp.bfloat16)
    query_cross_raw = product(second_low, query_full) + bias_vals[10]
    text_key_raw = product(text_rows, text_key_full) + bias_vals[11]
    text_value_raw = product(text_rows, text_value_full) + bias_vals[12]
    (cross_queries, text_keys), cross_pull = jax.vjp(
        cross_heads,
        query_cross_raw,
        text_key_raw,
        head_scales[2],
        head_shifts[2],
        head_scales[3],
    )
    cross_low = cross_queries.astype(jnp.bfloat16)
    text_key_low = text_keys.astype(jnp.bfloat16)
    text_value_low = head_view(text_value_raw).astype(jnp.bfloat16)
    cross_saved = []
    cross_parts = []
    for b in range(batches):
        part = (batch_of(cross_low, b), batch_of(text_key_low, b), batch_of(text_value_low, b))
        mixed, log_total = attend_forward(*part)
        cross_saved.append(part + (log_total,))
        cross_parts.append(mixed.astype(jnp.bfloat16))
    cross_out_low = jnp.concatenate(cross_parts, 0)
    hidden_three = hidden_two + product(cross_out_low, cross_out_full) + bias_vals[13]
    third_norm, third_pull = jax.vjp(layer_norm, hidden_three, gain_rows[4], bias_vals[14])
    third_low = third_norm.astype(jnp.bfloat16)
    result = hidden_three + bias_vals[15]
    gelu_lows, gelu_pulls = [], []
    for up_half, down_half, up_bias in zip(up_halves, down_halves, up_bias_halves):
        up_out = product(third_low, up_half) + up_bias
        gelu_val, gelu_pull = jax.vjp(partial(jax.nn.gelu, approximate=True), up_out)
        gelu_lows.append(gelu_val.astype(jnp.bfloat16))
        gelu_pulls.append(gelu_pull)
        result = result + product(gelu_lows[-1], down_half)
    activations = result.astype(jnp.bfloat16).reshape(latents.shape)

    def term(left_side, right_side):
        grads = weight_grad(left_side, right_side).astype(jnp.bfloat16)
        return grads.reshape(n, -1, grads.shape[-1])

    grad_low = out_cotangent.reshape(rows_all, D)
    grad_out = grad_low.astype(jnp.float32)
    grad_up_lows, grad_up_sums = [], []
    grad_third = None
    for up_half, down_half, gelu_pull in zip(up_halves, down_halves, gelu_pulls):
        grad_up = gelu_pull(back_product(grad_low, down_half))[0]
        grad_up_sums.append(jnp.sum(grad_up, 0))
        grad_up_lows.append(grad_up.astype(jnp.bfloat16))
        share = back_product(grad_up_lows[-1], up_half)
        grad_third = share if grad_third is None else grad_third + share
    down_terms = [term(gelu_low, grad_low) for gelu_low in gelu_lows]
    up_terms = [term(third_low, part) for part in grad_up_lows]
    three_part, gain_last, bias_last = third_pull(grad_third)
    grad_three = grad_out + three_part
    grad_three_low = grad_three.astype(jnp.bfloat16)
    cross_out_term = term(cross_out_low, grad_three_low)
    grad_cross_mixed = back_product(grad_three_low, cross_out_full).astype(jnp.bfloat16)
    pieces = [
        attend_backward(*cross_saved[b], head_view(batch_of(grad_cross_mixed, b)))
        for b in range(batches)
    ]
    grad_cq, grad_tk, grad_tv = (jnp.concatenate(list(part), 0) for part in zip(*pieces))
    grad_cq_raw, grad_tk_raw, cross_gain_grad, cross_bias_grad, text_gain_grad = cross_pull(
        (grad_cq, grad_tk)
    )
    grad_cq_low = grad_cq_raw.astype(jnp.bfloat16)
    query_term = term(second_low, grad_cq_low)
    grad_second = back_product(grad_cq_low, query_full)
    grad_tv_raw = grad_tv.reshape(grad_tv.shape[0], D)
    grad_tk_low = grad_tk_raw.astype(jnp.bfloat16)
    grad_tv_low = grad_tv_raw.astype(jnp.bfloat16)
    text_key_term = term(text_rows, grad_tk_low)
    text_value_term = term(text_rows, grad_tv_low)
    text_grad = back_product(grad_tk_low, text_key_full) + back_product(
        grad_tv_low, text_value_full
    )
    text_grad = lax.psum(text_grad.astype(jnp.bfloat16), "rep").astype(jnp.float32)
    two_part, gain_mid, bias_mid = second_pull(grad_second)
    grad_two = grad_three + two_part
    grad_two_low = grad_two.astype(jnp.bfloat16)
    proj_out_term = term(self_low, grad_two_low)
    small_term = jnp.concatenate(
        [proj_out_term, query_term, cross_out_term, text_key_term, text_value_term], 1
    )
    grad_self_mixed = back_product(grad_two_low, proj_out_full).astype(jnp.bfloat16)
    pieces = [
        attend_backward(*self_saved[b], head_view(batch_of(grad_self_mixed, b)))
        for b in range(batches)
    ]
    grad_query = jnp.concatenate([part[0] for part in pieces], 0)
    grad_slots = jnp.stack(
        [
            jnp.stack([part[j].reshape(rep_count, local_tokens, D) for part in pieces], 1)
            for j in (1, 2)
        ],
        1,
    ).astype(jnp.bfloat16)
    if links.ring:
        got = links.swap_core(jnp.stack([grad_slots[1], grad_slots[3]]))
        chip = total32(jnp.stack([grad_slots[0], grad_slots[2]]), got)
        got = links.swap_side(chip[1].astype(jnp.bfloat16))
        grad_keyval_own = total32(chip[0], got)
    else:
        grad_keyval_own = lax.psum_scatter(
            grad_slots, "rep", scatter_dimension=0, tiled=True
        )[0].astype(jnp.float32)
    grad_key_rows = grad_keyval_own[0].reshape(rows_all, D)
    grad_value_rows = grad_keyval_own[1].reshape(rows_all, D)
    (
        grad_q_raw,
        grad_k_raw,
        self_qgain_grad,
        self_qbias_grad,
        self_kgain_grad,
        self_kbias_grad,
    ) = self_pull((grad_query, head_view(grad_key_rows)))
    grad_proj = jnp.concatenate([grad_q_raw, grad_k_raw, grad_value_rows], axis=1)
    grad_proj_low = grad_proj.astype(jnp.bfloat16)
    in_term = term(first_low, grad_proj_low)
    grad_first = back_product(grad_proj_low, proj_in_full)
    shift_grads = jnp.sum(grad_first.reshape(batches, local_tokens, D), 1)
    one_part, gain_first, bias_first = first_pull(grad_first)
    grad_hidden = grad_two + one_part
    grad_hidden_low = grad_hidden.astype(jnp.bfloat16)
    skip_term = term(normed_low, grad_hidden_low)
    grad_normed = back_product(grad_hidden_low, skip_full)
    grad_joined, gain_cat_grad, bias_cat_grad = joined_pull(grad_normed)

    if links.ring:
        links.sent = []
        down_blocks, down_own = reduce_start_halved(links, *down_terms)
        up_blocks, up_own = reduce_start_halved(links, *up_terms)
        moved = run_steps(
            links,
            {
                "down": reduce_ring(links, down_blocks),
                "up": reduce_ring(links, up_blocks),
                "small": reduce_ring(links, reduce_start(links, small_term)),
                "in": reduce_ring(links, reduce_start(links, in_term)),
                "skip": reduce_ring(links, reduce_start(links, skip_term)),
            },
            ["down", "down", "up", "down", "up", "down", "up", "up"]
            + ["small"] * 4
            + ["in"] * 4
            + ["skip"] * 4,
        )
        down_first, down_second = reduce_finish_halved(
            links, down_terms[0], down_own, moved["down"]
        )
        up_first, up_second = reduce_finish_halved(links, up_terms[0], up_own, moved["up"])
        small_sum = reduce_finish(links, small_term, moved["small"])
        in_sum = reduce_finish(links, in_term, moved["in"])
        skip_sum = reduce_finish(links, skip_term, moved["skip"])
    else:

        def reduced(stack):
            part = lax.psum_scatter(
                stack.astype(jnp.float32), "shard", scatter_dimension=0, tiled=True
            )[0]
            return part.astype(jnp.bfloat16)

        def ordered(pair):
            first = jnp.where(links.side == 0, pair[0], pair[1])
            second = jnp.where(links.side == 0, pair[1], pair[0])
            return [
                lax.psum(reduced(part), "rep").astype(jnp.float32) for part in (first, second)
            ]

        down_first, down_second = ordered(down_terms)
        up_first, up_second = ordered(up_terms)
        small_sum, in_sum, skip_sum = (
            lax.psum(reduced(stack), "rep").astype(jnp.float32)
            for stack in (small_term, in_term, skip_term)
        )
    down_sum = jnp.concatenate([down_first, down_second], 0)
    up_sum = jnp.stack(
        [up_first.reshape(own_rows, n, slab), up_second.reshape(own_rows, n, slab)], 2
    ).reshape(own_rows, hidden_units)
    small_sums = [small_sum[low:high] for low, high in small_parts]
    keyval_sum = jnp.concatenate(small_sums[3:], 1)

    all_shifts = lax.all_gather(shift_grads, ("rep", "shard"), axis=0)
    all_shifts = jnp.sum(all_shifts.reshape(rep_count, n * batches, D), 0)
    shift_sum = lax.dot_general(
        silu_cols.astype(jnp.float32),
        all_shifts,
        (((0,), (0,)), ((), ())),
        precision=lax.Precision.HIGHEST,
    )

    up_bias_sum = jnp.stack(
        [
            jnp.where(links.side == 0, grad_up_sums[0], grad_up_sums[1]).reshape(n, slab),
            jnp.where(links.side == 0, grad_up_sums[1], grad_up_sums[0]).reshape(n, slab),
        ],
        1,
    )
    vector_terms = [
        gain_cat_grad,
        gain_first,
        gain_mid,
        gain_last,
        bias_cat_grad,
        jnp.sum(grad_hidden, 0),
        bias_first,
        jnp.sum(shift_grads, 0),
        jnp.sum(grad_proj, 0),
        jnp.sum(grad_two, 0),
        bias_mid,
        jnp.sum(grad_cq_raw, 0),
        jnp.sum(grad_tk_raw, 0),
        jnp.sum(grad_tv_raw, 0),
        jnp.sum(grad_three, 0),
        bias_last,
        jnp.sum(grad_out, 0),
        up_bias_sum.reshape(-1),
        self_qgain_grad,
        self_kgain_grad,
        cross_gain_grad,
        text_gain_grad,
        self_qbias_grad,
        self_kbias_grad,
        cross_bias_grad,
    ]
    summed = lax.psum(jnp.concatenate(vector_terms), ("rep", "shard"))
    line_count = norm_gains.shape[0] + bias_rows.shape[0]
    lines = summed[: line_count * D].reshape(line_count, D)
    own_lines = lax.dynamic_slice_in_dim(lines, links.shard * own_rows, own_rows, 1)
    rest = summed[line_count * D :]
    own_bias = lax.dynamic_slice_in_dim(rest[:hidden_units], links.shard * 2 * slab, 2 * slab, 0)
    heads = rest[hidden_units:].reshape(-1, HD)
    return (
        activations,
        grad_joined[:, :D].reshape(latents.shape),
        grad_joined[:, D:].reshape(latents.shape),
        text_grad.reshape(text_states.shape),
        skip_sum,
        shift_sum,
        in_sum,
        small_sums[0],
        small_sums[1],
        keyval_sum,
        small_sums[2],
        up_sum,
        down_sum,
        own_lines[: norm_gains.shape[0]],
        own_lines[norm_gains.shape[0] :],
        own_bias,
        heads[: head_gains.shape[0]],
        heads[head_gains.shape[0] :],
    )


def solution(mesh):
    in_specs = (
        P(None, "shard", "rep", None),
        P(None, "shard", "rep", None),
        P(None, "shard", None, None),
        P(None, "shard", None),
        P(None, "shard", "rep", None),
        P("shard", None),
        P("shard", None),
        P("shard", None),
        P("shard", None),
        P("shard", None),
        P("shard", None),
        P("shard", None),
        P("shard", None),
        P("shard", None),
        P(None, "shard"),
        P(None, "shard"),
        P("shard"),
        P(),
        P(),
    )
    out_specs = (
        P(None, "shard", "rep", None),
        P(None, "shard", "rep", None),
        P(None, "shard", "rep", None),
        P(None, "shard", None, None),
        P("shard", None),
        P("shard", None),
        P("shard", None),
        P("shard", None),
        P("shard", None),
        P("shard", None),
        P("shard", None),
        P("shard", None),
        P("shard", None),
        P(None, "shard"),
        P(None, "shard"),
        P("shard"),
        P(),
        P(),
    )
    block = partial(shards, mesh.shape["shard"], mesh.shape["rep"])
    return jax.shard_map(block, mesh=mesh, in_specs=in_specs, out_specs=out_specs, check_vma=False)
```

time: 4820 us -> 2390 us (0.50)
  waiting for transfers between devices: 3440 us -> 597 us
  local copies, waits for them, and re-layouts: 292 us -> 661 us
  other arithmetic: 226 us -> 426 us
  matrix products: 577 us -> 431 us
  blocking collectives: 183 us -> 80.9 us
  starting transfers between devices: 2.72 us -> 67 us
    reduce_scatter x13 -> x0, waiting for transfers between devices: 2160 us -> none  [the longest x1 554 us: shards(): lax.psum_scatter(totals[7], 'shard', scatter_dimension=0, tiled=True)]
    all_gather x13 -> x0, waiting for transfers between devices: 1040 us -> none  [the longest x1 314 us: shards(): lax.all_gather(feed_down, 'shard', axis=0, tiled=True)]
    ppermute x0 -> x79, waiting for transfers between devices: none -> 440 us  [the longest x40 235 us: along_ring(): moved = lax.ppermute(block, ('rep', 'shard'), self.ring_perm)]
    another operation x32 -> x37, local copies, waits for them, and re-layouts: 20.5 us -> 140 us  [the longest x8 51.3 us: shards(): jnp.stack([part[j].reshape(rep_count, local_tokens, D) for part in pieces...]
    dot_general x16 -> x11, matrix products: 166 us -> 75 us  [weight_grad(): lax.dot_general(left_side, right_side, (((0,), (0,)), ((), ())), preferre...]
    dynamic_update_slice x0 -> x57, local copies, waits for them, and re-layouts: none -> 90.7 us  [place(): return lax.dynamic_update_slice(stack, block[None], (index, row, 0))]
    slice x15 -> x32, local copies, waits for them, and re-layouts: 9.93 us -> 82.5 us  [the longest x3 32.8 us: shards(): keys_seq = head_view(slots[:, 0, b].reshape(-1, D))]
    another operation x2 -> x10, other arithmetic: 9.51 us -> 78.6 us  [the longest x3 40.9 us: shards(): jnp.stack([jnp.stack([part[j].reshape(rep_count, local_tokens, D) for par...]
  transfers between devices with their start and end apart: 29 -> 83, of which waited for: 18 -> 31; matrix products, arithmetic and copies ran while one was open for 16% -> 62% of each run, Pallas kernels for 0% -> 0%
where the time goes in v1:
time: 2390 us; the launch traced here: 2360 us
  local copies, waits for them, and re-layouts  661 us (28%)
  waiting for transfers between devices  597 us (25%)
  matrix products  431 us (18%)
  other arithmetic  426 us (18%)
  blocking collectives  80.9 us (3%)
  starting transfers between devices  67 us (3%)
  loops' own time  63.3 us (3%)
  between operations  37.2 us (2%)
    ppermute x40, waiting for transfers between devices, along_ring(): moved = lax.ppermute(block, ('rep', 'shard'), self.ring_perm)  235 us
    ppermute x13, waiting for transfers between devices, swap_side(): return lax.ppermute(block, 'rep', self.side_perm)  203 us
    psum x1, waiting for transfers between devices, shards(): summed = lax.psum(jnp.concatenate(vector_terms), ('rep', 'shard'))  117 us
    dot_general x11, matrix products, back_product(): lax.dot_general(grad_rows, weight, (((1,), (1,)), ((), ())), preferred_el...  94.5 us
    dynamic_update_slice x57, local copies, waits for them, and re-layouts, place(): return lax.dynamic_update_slice(stack, block[None], (index, row, 0))  90.7 us
    all_gather x1, blocking collectives, shards(): all_shifts = lax.all_gather(shift_grads, ('rep', 'shard'), axis=0)  80.9 us
    dot_general x12, matrix products, product(): return jnp.dot(left_side, right_side, preferred_element_type=jnp.float32)  76.8 us
    unnamed x606, local copies, waits for them, and re-layouts  76.6 us
  transfers between devices with their start and end apart: 83, of which 31 were waited for; matrix products, arithmetic and copies ran while one was open for 62% of the time, Pallas kernels for 0%

profile of v1, /device:TPU:0, one launch (start us, length us, event | category | flops | bytes accessed | tf_op | source)
XLA Modules:
  0.0 2363.5 jit_solution(3603734501607140542)
XLA Ops:
  47.8 9.6 dynamic-slice_reduce_fusion
  130.0 39.9 %all-reduce.27.cloned.1.call-done = f32[8,2,1408]{2,1,0:T(2,128)} async-done(((f32[8,2,1408]{2,1,0:T(2,128)}), f32[8,2,1408]{2,1,0:T(2,128)}) %all-reduce.27.cloned.1.call-update) | async-done | bytes 90128
  179.6 24.1 %collective-permute-done.3 = bf16[352,1408]{1,0:T(8,128)(2,1)S(1)} collective-permute-done((bf16[352,1408]{1,0:T(8,128)(2,1)S(1)}, bf16[352,1408]{1,0:T(8,128)(2,1)S(1)}, u32[]{:S(2)}, u32[]{:S(2)}) %collective-permute-start.3) | collective-permute-done | bytes 991264 | tf_op jit(solution)/shard_map/ppermute | solution.py:190
  214.4 14.3 collective-permute-done.9
  229.6 10.7 collective-permute-done.19
  267.0 28.1 %collective-permute-done.21 = bf16[176,3072]{1,0:T(8,128)(2,1)S(1)} collective-permute-done((bf16[176,3072]{1,0:T(8,128)(2,1)S(1)}, bf16[176,3072]{1,0:T(8,128)(2,1)S(1)}, u32[]{:S(2)}, u32[]{:S(2)}) %collective-permute-start.21) | collective-permute-done | bytes 1081376 | tf_op jit(solution)/shard_map/ppermute | solution.py:190
  493.7 24.7 %pad_maximum_fusion = bf16[4,2,2,256,1408]{3,2,4,1,0:T(2,128)(2,1)S(1)} fusion(bf16[1,2,2,256,1408]{3,2,4,1,0:T(2,128)(2,1)} %copy.285, bf16[1,2,2,256,1408]{3,2,4,1,0:T(2,128)(2,1)} %copy.284, bf16[1,2,2,256,1408]{3,2,4,1,0:T(2,128)(2,1)} %copy.283, bf16[1,1,2,256,1408]{3,2,4,1,0:T(2,128)(2,1)} %copy.281, ...), kind=kLoop, calls=%fused_computation.180 | loop fusion | flops 23068672 | bytes 23068672 | tf_op jit(solution)/shard_map/stack | solution.py:547
  518.4 19.2 fusion.360
  565.0 30.9 %while.105 = (s32[]{:T(128)}, bf16[4,256,4,88]{1,3,2,0:T(8,128)(2,1)S(1)}, f32[4,4,256]{2,1,0:T(4,128)S(1)}, s32[4]{0:T(128)S(1)}, bf16[1024,16,88]{0,2,1:T(8,12...) while((s32[]{:T(128)}, ...), condition=%wide.region_17.18_spmd, body=%wide.region_14.17_spmd.sunk | while | flops 378534912 | bytes 14599335 | solution.py:95
  622.4 34.9 %while.104 = (s32[]{:T(128)}, bf16[4,256,4,88]{1,3,2,0:T(8,128)(2,1)}, f32[4,4,256]{2,1,0:T(4,128)S(1)}, s32[4]{0:T(128)S(1)}, bf16[1024,16,88]{0,2,1:T(8,128)(2...) while((s32[]{:T(128)}, ...), condition=%wide.region_13.14_spmd, body=%wide.region_10.13_spmd.sunk | while | flops 378534912 | bytes 20366560 | solution.py:95
  691.2 19.3 collective-permute-done.31
  761.9 23.7 %while.107 = (s32[]{:T(128)}, bf16[4,256,4,88]{1,3,2,0:T(8,128)(2,1)}, f32[4,4,256]{2,1,0:T(4,128)S(1)}, s32[4]{0:T(128)S(1)}, bf16[256,16,88]{0,2,1:T(8,128)(2,...) while((s32[]{:T(128)}, ...), condition=%wide.region_31.32_spmd, body=%wide.region_28.31_spmd.sunk | while | flops 94108672 | bytes 4080807 | solution.py:95
  785.6 20.0 while.106
  827.8 11.5 fusion.380
  839.3 10.3 convolution_convert_fusion.2
  867.1 11.0 convolution_convert_fusion.1
  899.1 17.6 fusion.378
  924.9 12.7 fusion.379
  937.6 11.3 multiply_reduce_fusion.12
  959.3 38.3 %while.109 = (s32[]{:T(128)}, f32[4,256,4,88]{1,3,2,0:T(8,128)S(1)}, f32[4,256,4,88]{1,3,2,0:T(8,128)}, f32[4,256,4,88]{1,3,2,0:T(8,128)}, s32[4]{0:T(128)S(1)},...) while((s32[]{:T(128)}, f32[4,256,4,88]{1,3,2,0:T(8,128)S(1)}, ...), condition=%wide.region_41.42_spmd, body=%wide.region_39.41_spmd.sunk | while | flops 232963072 | bytes 10229967 | solution.py:139
  1004.2 41.2 %while.108 = (s32[]{:T(128)}, f32[4,256,4,88]{1,3,2,0:T(8,128)}, f32[4,256,4,88]{1,3,2,0:T(8,128)}, f32[4,256,4,88]{1,3,2,0:T(8,128)}, s32[4]{0:T(128)S(1)}, /*i...) while((s32[]{:T(128)}, f32[4,256,4,88]{1,3,2,0:T(8,128)}, ...), condition=%wide.region_38.39_spmd, body=%wide.region_36.38_spmd.sunk | while | flops 232963072 | bytes 10229967 | solution.py:139
  1122.3 61.0 %while.111 = (s32[]{:T(128)}, f32[4,256,4,88]{1,3,2,0:T(8,128)}, bf16[4,1024,4,88]{1,3,2,0:T(8,128)(2,1)}, bf16[4,1024,4,88]{1,3,2,0:T(8,128)(2,1)}, s32[4]{0:T(...) while((s32[]{:T(128)}, f32[4,256,4,88]{1,3,2,0:T(8,128)}, ...), condition=%wide.region_51.52_spmd, body=%wide.region_49.51_spmd.sunk | while | flops 935779328 | bytes 83753272 | solution.py:139
  1201.3 60.7 %while.110 = (s32[]{:T(128)}, f32[4,256,4,88]{1,3,2,0:T(8,128)}, bf16[4,1024,4,88]{1,3,2,0:T(8,128)(2,1)}, bf16[4,1024,4,88]{1,3,2,0:T(8,128)(2,1)}, s32[4]{0:T(...) while((s32[]{:T(128)}, f32[4,256,4,88]{1,3,2,0:T(8,128)}, ...), condition=%wide.region_48.49_spmd, body=%wide.region_46.48_spmd.sunk | while | flops 935779328 | bytes 83753272 | solution.py:139
  1300.7 14.5 maximum_bitcast_fusion.1
  1315.3 12.1 maximum_bitcast_fusion
  1327.5 14.3 fusion.181
  1377.6 19.1 pad_maximum_fusion.2
  1415.4 11.5 convolution_add_fusion.3
  1430.7 11.7 fusion.174
  1464.6 8.8 convert_add_fusion
  1491.6 79.3 %collective-permute-done.45 = bf16[1728,1408]{1,0:T(8,128)(2,1)S(1)} collective-permute-done((bf16[1728,1408]{1,0:T(8,128)(2,1)S(1)}, bf16[1728,1408]{1,0:T(8,128)(2,1)S(1)}, u32[]{:S(2)}, u32[]{:S(2)}) %collective-permute-start.45) | collective-permute-done | bytes 4866080 | tf_op jit(solution)/shard_map/ppermute | solution.py:198
  1574.0 58.6 %collective-permute-done.38 = bf16[2,2,256,1408]{2,1,3,0:T(2,128)(2,1)S(1)} collective-permute-done((bf16[2,2,256,1408]{2,1,3,0:T(2,128)(2,1)S(1)}, bf16[2,2,256,1408]{2,1,3,0:T(2,128)(2,1)S(1)}, u32[]{:S(2)}, u32[]{:S(2)}) %collective-permute-start.38) | collective-permute-done | bytes 2883616 | tf_op jit(solution)/shard_map/ppermute | solution.py:198
  1645.5 9.7 multiply_add_fusion.5
  1691.5 8.9 multiply_reduce_fusion.11
  1719.6 8.9 multiply_reduce_fusion.10
  1742.6 14.3 fusion.185
  1756.9 15.6 multiply_reduce_fusion.14
  1787.2 14.9 convolution_convert_fusion
  1872.3 10.7 collective-permute-done.50
  1898.4 11.3 multiply_reduce_fusion.6
  1930.9 22.4 collective-permute-done.56
  1962.1 29.6 %collective-permute-done.57 = bf16[88,4224]{1,0:T(8,128)(2,1)S(1)} collective-permute-done((bf16[88,4224]{1,0:T(8,128)(2,1)S(1)}, bf16[88,4224]{1,0:T(8,128)(2,1)S(1)}, u32[]{:S(2)}, u32[]{:S(2)}) %collective-permute-start.57) | collective-permute-done | bytes 743456 | tf_op jit(solution)/shard_map/ppermute | solution.py:190
  1995.8 80.9 %all-gather.2 = f32[32,2,1408]{2,1,0:T(2,128)S(1)} all-gather(f32[1,2,1408]{2,1,0:T(2,128)S(1)} %bitcast.1198), channel_id=3, replica_groups=mesh['rep'=4,'shard'=8] {'rep','shard'}, dimensions={0}, use_global_device_ids=true | all-gather | bytes 371712 | tf_op jit(solution)/shard_map/all_gather | solution.py:749
  2080.7 117.3 %all-reduce.23.cloned.1.call-done = f32[36328]{0:T(1024)} async-done(((f32[36328]{0:T(1024)}), f32[36328]{0:T(1024)}) %all-reduce.23.cloned.1.call-update) | async-done | bytes 145328 | tf_op jit(solution)/shard_map/psum | solution.py:792
  2216.3 17.6 collective-permute-done.78
  2251.8 12.8 collective-permute-done.62
  2312.0 9.6 collective-permute-done.65
  2326.3 16.6 collective-permute-done.70
  (1534 shorter events, 1368.2 us)
Async XLA Ops:
  7.2 86.3 %all-reduce.25.cloned.1.call-start = ((), (), s32[]{:S(2)}) async-start(), calls=%async_computation.2 | async-start | bytes 233472
  7.2 166.2 %collective-permute-start.6 = (bf16[176,4224]{1,0:T(8,128)(2,1)}, bf16[176,4224]{1,0:T(8,128)(2,1)}, u32[]{:S(2)}, u32[]{:S(2)}) collective-permute-start(bf16[176,4224]{1,0:T(8,128)(2,1)} %param.44), channel_id=1, source_target_pairs={{0,2},{2,4},{4,6},{6,7},{7,5},{5,3},{3,1},{1,0},{8,9},{10,8},{12,1... | collective-permute-start | bytes 4460552 | tf_op jit(solution)/shard_map/ppermute | solution.py:190
  10.4 90.5 %collective-permute-start = (bf16[352,1408]{1,0:T(8,128)(2,1)}, bf16[352,1408]{1,0:T(8,128)(2,1)}, u32[]{:S(2)}, u32[]{:S(2)}) collective-permute-start(bf16[352,1408]{1,0:T(8,128)(2,1)} %param.42), channel_id=1, source_target_pairs={{0,2},{2,4},{4,6},{6,7},{7,5},{5,3},{3,1},{1,0},{8,9},{10,8},{12,1... | collective-permute-start | bytes 2973704 | tf_op jit(solution)/shard_map/ppermute | solution.py:190
  18.1 151.7 %all-reduce.27.cloned.1.call-start = ((), (), s32[]{:S(2)}) async-start(), calls=%async_computation.3 | async-start | bytes 180224
  100.2 1350.9 %all-reduce.21.cloned.1.call-start = ((), (), s32[]{:S(2)}) async-start(), calls=%async_computation | async-start | bytes 2097152 | tf_op jit(solution)/shard_map/psum | solution.py:644
  100.9 73.3 %collective-permute-start.1 = (bf16[352,1408]{1,0:T(8,128)(2,1)}, bf16[352,1408]{1,0:T(8,128)(2,1)S(1)}, u32[]{:S(2)}, u32[]{:S(2)}) collective-permute-start(bf16[352,1408]{1,0:T(8,128)(2,1)} %collective-permute-done), channel_id=1, source_target_pairs={{0,2},{2,4},{4,6},{6,7},{7,5},{5,3},{3,1},{1,0},{8,9},{10,8},{12,1... | collective-permute-start | bytes 2973704 | tf_op jit(solution)/shard_map/ppermute | solution.py:190
  173.4 31.3 %collective-permute-start.7 = (bf16[176,4224]{1,0:T(8,128)(2,1)}, bf16[176,4224]{1,0:T(8,128)(2,1)S(1)}, u32[]{:S(2)}, u32[]{:S(2)}) collective-permute-start(bf16[176,4224]{1,0:T(8,128)(2,1)} %collective-permute-done.6), channel_id=1, source_target_pairs={{0,2},{2,4},{4,6},{6,7},{7,5},{5,3},{3,1},{1,0},{8,9},{10,8},{12,1... | collective-permute-start | bytes 4460552 | tf_op jit(solution)/shard_map/ppermute | solution.py:190
  174.2 29.5 %collective-permute-start.3 = (bf16[352,1408]{1,0:T(8,128)(2,1)S(1)}, bf16[352,1408]{1,0:T(8,128)(2,1)S(1)}, u32[]{:S(2)}, u32[]{:S(2)}) collective-permute-start(bf16[352,1408]{1,0:T(8,128)(2,1)S(1)} %collective-permute-done.1), channel_id=1, source_target_pairs={{0,2},{2,4},{4,6},{6,7},{7,5},{5,3},{3,1},{1,0},{8,9},{10,8},{12,1... | collective-permute-start | bytes 2973704 | tf_op jit(solution)/shard_map/ppermute | solution.py:190
  176.9 36.8 %collective-permute-start.2 = (bf16[704,1408]{1,0:T(8,128)(2,1)S(1)}, bf16[704,1408]{1,0:T(8,128)(2,1)S(1)}, u32[]{:S(2)}, u32[]{:S(2)}) collective-permute-start(bf16[704,1408]{1,0:T(8,128)(2,1)S(1)} %pad_maximum_fusion.19), channel_id=1, source_target_pairs={{0,8},{8,0},{16,24},{24,16},{1,9},{9,1},{17,25},{25,17},{2,10},{10... | collective-permute-start | bytes 5947400 | tf_op jit(solution)/shard_map/ppermute | solution.py:195
  209.1 54.5 %collective-permute-start.8 = (bf16[352,4224]{1,0:T(8,128)(2,1)}, bf16[352,4224]{1,0:T(8,128)(2,1)}, u32[]{:S(2)}, u32[]{:S(2)}) collective-permute-start(bf16[352,4224]{1,0:T(8,128)(2,1)} %pad_maximum_fusion.11), channel_id=1, source_target_pairs={{0,8},{8,0},{16,24},{24,16},{1,9},{9,1},{17,25},{25,17},{2,10},{10... | collective-permute-start | bytes 8921096 | tf_op jit(solution)/shard_map/ppermute | solution.py:195
  212.7 27.5 %collective-permute-start.19 = (bf16[176,3072]{1,0:T(8,128)(2,1)S(1)}, bf16[176,3072]{1,0:T(8,128)(2,1)S(1)}, u32[]{:S(2)}, u32[]{:S(2)}) collective-permute-start(bf16[176,3072]{1,0:T(8,128)(2,1)S(1)} %bitcast.1180), channel_id=1, source_target_pairs={{0,2},{2,4},{4,6},{6,7},{7,5},{5,3},{3,1},{1,0},{8,9},{10,8},{12,1... | collective-permute-start | bytes 3244040 | tf_op jit(solution)/shard_map/ppermute | solution.py:190
  213.7 28.7 %collective-permute-start.5 = (bf16[528,1408]{1,0:T(8,128)(2,1)S(1)}, bf16[528,1408]{1,0:T(8,128)(2,1)S(1)}, u32[]{:S(2)}, u32[]{:S(2)}) collective-permute-start(bf16[528,1408]{1,0:T(8,128)(2,1)S(1)} %pad_maximum_fusion.22), channel_id=1, source_target_pairs={{0,8},{8,0},{16,24},{24,16},{1,9},{9,1},{17,25},{25,17},{2,10},{10... | collective-permute-start | bytes 4460552 | tf_op jit(solution)/shard_map/ppermute | solution.py:195
  251.8 55.4 %collective-permute-start.15 = (bf16[784,1408]{1,0:T(8,128)(2,1)}, bf16[784,1408]{1,0:T(8,128)(2,1)}, u32[]{:S(2)}, u32[]{:S(2)}) collective-permute-start(bf16[784,1408]{1,0:T(8,128)(2,1)} %slice_dynamic-update-slice_fusion), channel_id=1, source_target_pairs={{0,2},{2,4},{4,6},{6,7},{7,5},{5,3},{3,1},{1,0},{8,9},{10,8},{12,1... | collective-permute-start | bytes 6623240 | tf_op jit(solution)/shard_map/ppermute | solution.py:190
  253.2 59.8 %collective-permute-start.11 = (bf16[264,4224]{1,0:T(8,128)(2,1)S(1)}, bf16[264,4224]{1,0:T(8,128)(2,1)S(1)}, u32[]{:S(2)}, u32[]{:S(2)}) collective-permute-start(bf16[264,4224]{1,0:T(8,128)(2,1)S(1)} %pad_maximum_fusion.16), channel_id=1, source_target_pairs={{0,8},{8,0},{16,24},{24,16},{1,9},{9,1},{17,25},{25,17},{2,10},{10... | collective-permute-start | bytes 6690824 | tf_op jit(solution)/shard_map/ppermute | solution.py:195
  259.8 35.2 %collective-permute-start.21 = (bf16[176,3072]{1,0:T(8,128)(2,1)S(1)}, bf16[176,3072]{1,0:T(8,128)(2,1)S(1)}, u32[]{:S(2)}, u32[]{:S(2)}) collective-permute-start(bf16[176,3072]{1,0:T(8,128)(2,1)S(1)} %collective-permute-done.20), channel_id=1, source_target_pairs={{0,2},{2,4},{4,6},{6,7},{7,5},{5,3},{3,1},{1,0},{8,9},{10,8},{12,1... | collective-permute-start | bytes 3244040 | tf_op jit(solution)/shard_map/ppermute | solution.py:190
  262.1 108.7 %collective-permute-start.25 = (bf16[352,3072]{1,0:T(8,128)(2,1)}, bf16[352,3072]{1,0:T(8,128)(2,1)}, u32[]{:S(2)}, u32[]{:S(2)}) collective-permute-start(bf16[352,3072]{1,0:T(8,128)(2,1)} %pad_maximum_fusion.17), channel_id=1, source_target_pairs={{0,16},{8,24},{16,0},{24,8},{1,17},{9,25},{17,1},{25,9},{2,18},{10... | collective-permute-start | bytes 6488072 | tf_op jit(solution)/shard_map/ppermute | solution.py:198
  305.8 120.7 %collective-permute-start.27 = (bf16[264,3072]{1,0:T(8,128)(2,1)}, bf16[264,3072]{1,0:T(8,128)(2,1)}, u32[]{:S(2)}, u32[]{:S(2)}) collective-permute-start(bf16[264,3072]{1,0:T(8,128)(2,1)} %pad_maximum_fusion.20), channel_id=1, source_target_pairs={{0,16},{8,24},{16,0},{24,8},{1,17},{9,25},{17,1},{25,9},{2,18},{10... | collective-permute-start | bytes 4866056 | tf_op jit(solution)/shard_map/ppermute | solution.py:198
  307.2 115.5 %collective-permute-start.16 = (bf16[784,1408]{1,0:T(8,128)(2,1)}, bf16[784,1408]{1,0:T(8,128)(2,1)}, u32[]{:S(2)}, u32[]{:S(2)}) collective-permute-start(bf16[784,1408]{1,0:T(8,128)(2,1)} %collective-permute-done.15), channel_id=1, source_target_pairs={{0,2},{2,4},{4,6},{6,7},{7,5},{5,3},{3,1},{1,0},{8,9},{10,8},{12,1... | collective-permute-start | bytes 6623240 | tf_op jit(solution)/shard_map/ppermute | solution.py:190
  356.5 79.6 %collective-permute-start.13 = (bf16[2,512,1408]{2,1,0:T(8,128)(2,1)}, bf16[2,512,1408]{2,1,0:T(8,128)(2,1)}, u32[]{:S(2)}, u32[]{:S(2)}) collective-permute-start(bf16[2,512,1408]{2,1,0:T(8,128)(2,1)} %pad_maximum_fusion.13), channel_id=1, source_target_pairs={{0,16},{8,24},{16,0},{24,8},{1,17},{9,25},{17,1},{25,9},{2,18},{10... | collective-permute-start | bytes 8650760 | tf_op jit(solution)/shard_map/ppermute | solution.py:198
  357.1 87.6 %collective-permute-start.12 = (bf16[2,512,1408]{2,1,0:T(8,128)(2,1)}, bf16[2,512,1408]{2,1,0:T(8,128)(2,1)}, u32[]{:S(2)}, u32[]{:S(2)}) collective-permute-start(bf16[2,512,1408]{2,1,0:T(8,128)(2,1)} %pad_maximum_fusion.13), channel_id=1, source_target_pairs={{0,8},{8,0},{16,24},{24,16},{1,9},{9,1},{17,25},{25,17},{2,10},{10... | collective-permute-start | bytes 8650760 | tf_op jit(solution)/shard_map/ppermute | solution.py:195
  374.7 80.8 %collective-permute-start.26 = (bf16[704,3072]{1,0:T(8,128)(2,1)}, bf16[704,3072]{1,0:T(8,128)(2,1)}, u32[]{:S(2)}, u32[]{:S(2)}) collective-permute-start(bf16[704,3072]{1,0:T(8,128)(2,1)} %pad_maximum_fusion.5), channel_id=1, source_target_pairs={{0,8},{8,0},{16,24},{24,16},{1,9},{9,1},{17,25},{25,17},{2,10},{10... | collective-permute-start | bytes 12976136 | tf_op jit(solution)/shard_map/ppermute | solution.py:195
  422.8 29.9 %collective-permute-start.18 = (bf16[784,1408]{1,0:T(8,128)(2,1)}, bf16[784,1408]{1,0:T(8,128)(2,1)}, u32[]{:S(2)}, u32[]{:S(2)}) collective-permute-start(bf16[784,1408]{1,0:T(8,128)(2,1)} %collective-permute-done.16), channel_id=1, source_target_pairs={{0,2},{2,4},{4,6},{6,7},{7,5},{5,3},{3,1},{1,0},{8,9},{10,8},{12,1... | collective-permute-start | bytes 6623240 | tf_op jit(solution)/shard_map/ppermute | solution.py:190
  429.5 41.2 %collective-permute-start.28 = (bf16[528,3072]{1,0:T(8,128)(2,1)}, bf16[528,3072]{1,0:T(8,128)(2,1)}, u32[]{:S(2)}, u32[]{:S(2)}) collective-permute-start(bf16[528,3072]{1,0:T(8,128)(2,1)} %pad_maximum_fusion.9), channel_id=1, source_target_pairs={{0,8},{8,0},{16,24},{24,16},{1,9},{9,1},{17,25},{25,17},{2,10},{10... | collective-permute-start | bytes 9732104 | tf_op jit(solution)/shard_map/ppermute | solution.py:195
  436.1 226.7 %collective-permute-start.17 = (bf16[1568,1408]{1,0:T(8,128)(2,1)}, bf16[1568,1408]{1,0:T(8,128)(2,1)}, u32[]{:S(2)}, u32[]{:S(2)}) collective-permute-start(bf16[1568,1408]{1,0:T(8,128)(2,1)} %pad_maximum_fusion.4), channel_id=1, source_target_pairs={{0,8},{8,0},{16,24},{24,16},{1,9},{9,1},{17,25},{25,17},{2,10},{10... | collective-permute-start | bytes 13246472 | tf_op jit(solution)/shard_map/ppermute | solution.py:195
  452.7 33.0 %collective-permute-start.14 = (bf16[2,512,1408]{2,1,0:T(8,128)(2,1)}, bf16[2,512,1408]{2,1,0:T(8,128)(2,1)}, u32[]{:S(2)}, u32[]{:S(2)}) collective-permute-start(bf16[2,512,1408]{2,1,0:T(8,128)(2,1)} %collective-permute-done.13), channel_id=1, source_target_pairs={{0,8},{8,0},{16,24},{24,16},{1,9},{9,1},{17,25},{25,17},{2,10},{10... | collective-permute-start | bytes 8650760 | tf_op jit(solution)/shard_map/ppermute | solution.py:195
  477.6 180.9 %collective-permute-start.30 = (bf16[384,1408]{1,0:T(8,128)(2,1)}, bf16[384,1408]{1,0:T(8,128)(2,1)}, u32[]{:S(2)}, u32[]{:S(2)}) collective-permute-start(bf16[384,1408]{1,0:T(8,128)(2,1)} %collective-permute-done.29), channel_id=1, source_target_pairs={{0,2},{2,4},{4,6},{6,7},{7,5},{5,3},{3,1},{1,0},{8,9},{10,8},{12,1... | collective-permute-start | bytes 3244040 | tf_op jit(solution)/shard_map/ppermute | solution.py:190
  485.6 230.6 %collective-permute-start.24 = (bf16[1176,1408]{1,0:T(8,128)(2,1)}, bf16[1176,1408]{1,0:T(8,128)(2,1)}, u32[]{:S(2)}, u32[]{:S(2)}) collective-permute-start(bf16[1176,1408]{1,0:T(8,128)(2,1)} %pad_maximum_fusion.8), channel_id=1, source_target_pairs={{0,8},{8,0},{16,24},{24,16},{1,9},{9,1},{17,25},{25,17},{2,10},{10... | collective-permute-start | bytes 9934856 | tf_op jit(solution)/shard_map/ppermute | solution.py:195
  660.5 50.0 %collective-permute-start.31 = (bf16[768,1408]{1,0:T(8,128)(2,1)S(1)}, bf16[768,1408]{1,0:T(8,128)(2,1)S(1)}, u32[]{:S(2)}, u32[]{:S(2)}) collective-permute-start(bf16[768,1408]{1,0:T(8,128)(2,1)S(1)} %pad_maximum_fusion.18), channel_id=1, source_target_pairs={{0,16},{8,24},{16,0},{24,8},{1,17},{9,25},{17,1},{25,9},{2,18},{10... | collective-permute-start | bytes 6488072 | tf_op jit(solution)/shard_map/ppermute | solution.py:198
  690.6 172.4 %collective-permute-start.35 = (bf16[576,1408]{1,0:T(8,128)(2,1)}, bf16[576,1408]{1,0:T(8,128)(2,1)}, u32[]{:S(2)}, u32[]{:S(2)}) collective-permute-start(bf16[576,1408]{1,0:T(8,128)(2,1)} %pad_maximum_fusion.21), channel_id=1, source_target_pairs={{0,16},{8,24},{16,0},{24,8},{1,17},{9,25},{17,1},{25,9},{2,18},{10... | collective-permute-start | bytes 4866056 | tf_op jit(solution)/shard_map/ppermute | solution.py:198
  715.2 169.5 %collective-permute-start.32 = (bf16[1536,1408]{1,0:T(8,128)(2,1)}, bf16[1536,1408]{1,0:T(8,128)(2,1)}, u32[]{:S(2)}, u32[]{:S(2)}) collective-permute-start(bf16[1536,1408]{1,0:T(8,128)(2,1)} %pad_maximum_fusion.6), channel_id=1, source_target_pairs={{0,8},{8,0},{16,24},{24,16},{1,9},{9,1},{17,25},{25,17},{2,10},{10... | collective-permute-start | bytes 12976136 | tf_op jit(solution)/shard_map/ppermute | solution.py:195
  883.3 570.5 %collective-permute-start.44 = (bf16[2688,1408]{1,0:T(8,128)(2,1)}, bf16[2688,1408]{1,0:T(8,128)(2,1)}, u32[]{:S(2)}, u32[]{:S(2)}) collective-permute-start(bf16[2688,1408]{1,0:T(8,128)(2,1)} %bitcast_dynamic-update-slice_fusion.34), channel_id=1, source_target_pairs={{0,8},{8,0},{16,24},{24,16},{1,9},{9,1},{17,25},{25,17},{2,10},{10... | collective-permute-start | bytes 22708232 | tf_op jit(solution)/shard_map/ppermute | solution.py:195
  1347.7 116.9 %collective-permute-start.37 = (bf16[2,2,2,256,1408]{3,2,4,1,0:T(2,128)(2,1)}, bf16[2,2,2,256,1408]{3,2,4,1,0:T(2,128)(2,1)}, u32[]{:S(2)}, u32[]{:S(2)}) collective-permute-start(bf16[2,2,2,256,1408]{3,2,4,1,0:T(2,128)(2,1)} %fusion.165), channel_id=1, source_target_pairs={{0,8},{8,0},{16,24},{24,16},{1,9},{9,1},{17,25},{25,17},{2,10},{10... | collective-permute-start | bytes 17301512 | tf_op jit(solution)/shard_map/ppermute | solution.py:195
  1362.0 836.0 %all-reduce.23.cloned.1.call-start = ((), (), s32[]{:S(2)}) async-start(), calls=%async_computation.1 | async-start | bytes 294912 | tf_op jit(solution)/shard_map/psum | solution.py:792
  1396.7 91.9 %collective-permute-start.41 = (bf16[2744,1408]{1,0:T(8,128)(2,1)}, bf16[2744,1408]{1,0:T(8,128)(2,1)}, u32[]{:S(2)}, u32[]{:S(2)}) collective-permute-start(bf16[2744,1408]{1,0:T(8,128)(2,1)} %pad_maximum_fusion.2), channel_id=1, source_target_pairs={{0,8},{8,0},{16,24},{24,16},{1,9},{9,1},{17,25},{25,17},{2,10},{10... | collective-permute-start | bytes 23181320 | tf_op jit(solution)/shard_map/ppermute | solution.py:195
  1428.9 47.1 %collective-permute-start.42 = (bf16[1232,3072]{1,0:T(8,128)(2,1)}, bf16[1232,3072]{1,0:T(8,128)(2,1)}, u32[]{:S(2)}, u32[]{:S(2)}) collective-permute-start(bf16[1232,3072]{1,0:T(8,128)(2,1)} %bitcast_dynamic-update-slice_fusion.36), channel_id=1, source_target_pairs={{0,8},{8,0},{16,24},{24,16},{1,9},{9,1},{17,25},{25,17},{2,10},{10... | collective-permute-start | bytes 22708232 | tf_op jit(solution)/shard_map/ppermute | solution.py:195
  1462.9 107.9 %collective-permute-start.45 = (bf16[1728,1408]{1,0:T(8,128)(2,1)S(1)}, bf16[1728,1408]{1,0:T(8,128)(2,1)S(1)}, u32[]{:S(2)}, u32[]{:S(2)}) collective-permute-start(bf16[1728,1408]{1,0:T(8,128)(2,1)S(1)} %bitcast_dynamic-update-slice_fusion.8), channel_id=1, source_target_pairs={{0,16},{8,24},{16,0},{24,8},{1,17},{9,25},{17,1},{25,9},{2,18},{10... | collective-permute-start | bytes 14598152 | tf_op jit(solution)/shard_map/ppermute | solution.py:198
  1475.5 157.1 %collective-permute-start.38 = (bf16[2,2,256,1408]{2,1,3,0:T(2,128)(2,1)S(1)}, bf16[2,2,256,1408]{2,1,3,0:T(2,128)(2,1)S(1)}, u32[]{:S(2)}, u32[]{:S(2)}) collective-permute-start(bf16[2,2,256,1408]{2,1,3,0:T(2,128)(2,1)S(1)} %fusion.193), channel_id=1, source_target_pairs={{0,16},{8,24},{16,0},{24,8},{1,17},{9,25},{17,1},{25,9},{2,18},{10... | collective-permute-start | bytes 8650760 | tf_op jit(solution)/shard_map/ppermute | solution.py:198
  1487.0 315.1 %collective-permute-start.43 = (bf16[792,3072]{1,0:T(8,128)(2,1)}, bf16[792,3072]{1,0:T(8,128)(2,1)}, u32[]{:S(2)}, u32[]{:S(2)}) collective-permute-start(bf16[792,3072]{1,0:T(8,128)(2,1)} %bitcast_dynamic-update-slice_fusion.15), channel_id=1, source_target_pairs={{0,16},{8,24},{16,0},{24,8},{1,17},{9,25},{17,1},{25,9},{2,18},{10... | collective-permute-start | bytes 14598152 | tf_op jit(solution)/shard_map/ppermute | solution.py:198
  1573.1 230.7 %collective-permute-start.46 = (bf16[192,1408]{1,0:T(8,128)(2,1)S(1)}, bf16[192,1408]{1,0:T(8,128)(2,1)}, u32[]{:S(2)}, u32[]{:S(2)}) collective-permute-start(bf16[192,1408]{1,0:T(8,128)(2,1)S(1)} %add_convert_fusion.33), channel_id=1, source_target_pairs={{0,2},{2,4},{4,6},{6,7},{7,5},{5,3},{3,1},{1,0},{8,9},{10,8},{12,1... | collective-permute-start | bytes 1622024 | tf_op jit(solution)/shard_map/ppermute | solution.py:190
  1836.3 368.2 %collective-permute-start.39 = (bf16[1232,1408]{1,0:T(8,128)(2,1)}, bf16[1232,1408]{1,0:T(8,128)(2,1)}, u32[]{:S(2)}, u32[]{:S(2)}) collective-permute-start(bf16[1232,1408]{1,0:T(8,128)(2,1)} %pad_maximum_fusion.7), channel_id=1, source_target_pairs={{0,8},{8,0},{16,24},{24,16},{1,9},{9,1},{17,25},{25,17},{2,10},{10... | collective-permute-start | bytes 10407944 | tf_op jit(solution)/shard_map/ppermute | solution.py:195
  1894.5 27.7 %collective-permute-start.55 = (bf16[784,1408]{1,0:T(8,128)(2,1)}, bf16[784,1408]{1,0:T(8,128)(2,1)}, u32[]{:S(2)}, u32[]{:S(2)}) collective-permute-start(bf16[784,1408]{1,0:T(8,128)(2,1)} %add_convert_fusion.3), channel_id=1, source_target_pairs={{0,2},{2,4},{4,6},{6,7},{7,5},{5,3},{3,1},{1,0},{8,9},{10,8},{12,1... | collective-permute-start | bytes 6623240 | tf_op jit(solution)/shard_map/ppermute | solution.py:190
  1898.4 59.1 %collective-permute-start.40 = (bf16[616,4224]{1,0:T(8,128)(2,1)}, bf16[616,4224]{1,0:T(8,128)(2,1)}, u32[]{:S(2)}, u32[]{:S(2)}) collective-permute-start(bf16[616,4224]{1,0:T(8,128)(2,1)} %pad_maximum_fusion.3), channel_id=1, source_target_pairs={{0,8},{8,0},{16,24},{24,16},{1,9},{9,1},{17,25},{25,17},{2,10},{10... | collective-permute-start | bytes 15611912 | tf_op jit(solution)/shard_map/ppermute | solution.py:195
  1956.5 38.3 %collective-permute-start.58 = (bf16[784,1408]{1,0:T(8,128)(2,1)S(1)}, bf16[784,1408]{1,0:T(8,128)(2,1)}, u32[]{:S(2)}, u32[]{:S(2)}) collective-permute-start(bf16[784,1408]{1,0:T(8,128)(2,1)S(1)} %add_convert_fusion.1), channel_id=1, source_target_pairs={{0,2},{2,4},{4,6},{6,7},{7,5},{5,3},{3,1},{1,0},{8,9},{10,8},{12,1... | collective-permute-start | bytes 6623240 | tf_op jit(solution)/shard_map/ppermute | solution.py:190
  1958.9 32.9 %collective-permute-start.57 = (bf16[88,4224]{1,0:T(8,128)(2,1)S(1)}, bf16[88,4224]{1,0:T(8,128)(2,1)S(1)}, u32[]{:S(2)}, u32[]{:S(2)}) collective-permute-start(bf16[88,4224]{1,0:T(8,128)(2,1)S(1)} %fusion.232), channel_id=1, source_target_pairs={{0,2},{2,4},{4,6},{6,7},{7,5},{5,3},{3,1},{1,0},{8,9},{10,8},{12,1... | collective-permute-start | bytes 2230280 | tf_op jit(solution)/shard_map/ppermute | solution.py:190
  1962.1 243.8 %collective-permute-start.77 = (bf16[384,1408]{1,0:T(8,128)(2,1)S(1)}, bf16[384,1408]{1,0:T(8,128)(2,1)}, u32[]{:S(2)}, u32[]{:S(2)}) collective-permute-start(bf16[384,1408]{1,0:T(8,128)(2,1)S(1)} %fusion.203), channel_id=1, source_target_pairs={{0,8},{8,0},{16,24},{24,16},{1,9},{9,1},{17,25},{25,17},{2,10},{10... | collective-permute-start | bytes 3244040 | tf_op jit(solution)/shard_map/ppermute | solution.py:195
  1994.9 214.0 %collective-permute-start.59 = (bf16[176,4224]{1,0:T(8,128)(2,1)}, bf16[176,4224]{1,0:T(8,128)(2,1)}, u32[]{:S(2)}, u32[]{:S(2)}) collective-permute-start(bf16[176,4224]{1,0:T(8,128)(2,1)} %add_convert_fusion.6), channel_id=1, source_target_pairs={{0,2},{2,4},{4,6},{6,7},{7,5},{5,3},{3,1},{1,0},{8,9},{10,8},{12,1... | collective-permute-start | bytes 4460552 | tf_op jit(solution)/shard_map/ppermute | solution.py:190
  2211.7 28.0 %collective-permute-start.60 = (bf16[176,4224]{1,0:T(8,128)(2,1)S(1)}, bf16[176,4224]{1,0:T(8,128)(2,1)S(1)}, u32[]{:S(2)}, u32[]{:S(2)}) collective-permute-start(bf16[176,4224]{1,0:T(8,128)(2,1)S(1)} %add_convert_fusion.5), channel_id=1, source_target_pairs={{0,2},{2,4},{4,6},{6,7},{7,5},{5,3},{3,1},{1,0},{8,9},{10,8},{12,1... | collective-permute-start | bytes 4460552 | tf_op jit(solution)/shard_map/ppermute | solution.py:190
  2266.0 37.1 %collective-permute-start.73 = (bf16[392,1408]{1,0:T(8,128)(2,1)}, bf16[392,1408]{1,0:T(8,128)(2,1)}, u32[]{:S(2)}, u32[]{:S(2)}) collective-permute-start(bf16[392,1408]{1,0:T(8,128)(2,1)} %add_convert_fusion.11), channel_id=1, source_target_pairs={{0,16},{8,24},{16,0},{24,8},{1,17},{9,25},{17,1},{25,9},{2,18},{10... | collective-permute-start | bytes 3311624 | tf_op jit(solution)/shard_map/ppermute | solution.py:198
  (361 other events, 6763.6 us)
Sparse Core Ops, SparseCore 0:
  18.2 69.1 all-reduce.24
  100.3 69.4 all-reduce.26
  1362.1 34.8 all-reduce.20
  2078.5 119.4 all-reduce.22
